TPU v7x, 512 devices: a whole 4x8x8 slice. The times are simulated.
512 devices in a mesh: dp: 8 (over y), row: 4 (over x), col: 16 (over z, core).
Axes of the slice: x: 4, y: 8, z: 8, core: 2. Of those that a mesh axis runs over, the one named last changes fastest.
Arguments:
- tokens: bfloat16 [8192, 8192], P(('dp', 'col'), 'row'), may hold values from -6 to 6
- frozen_weight: bfloat16 [8192, 8192], P('row', 'col'), may hold values from -0.0625 to 0.0625
- input_adapter_factor: bfloat16 [16, 8192], P(None, 'row'), may hold values from -0.0625 to 0.0625
- output_adapter_factor: bfloat16 [16, 8192], P(None, 'col'), may hold values from -1.5 to 1.5
- magnitude: float32 [8192], P('col'), may hold values from 0.5 to 2
- cotangent: bfloat16 [8192, 8192], P(('dp', 'row'), 'col'), may hold values from -6 to 6
- sequence_lengths: int32 [8, 8], P('dp'), may hold values from 1 to 512, 1024 in all within a row
Outputs:
- projected: bfloat16 [8192, 8192], P(('dp', 'row'), 'col')
- grad_mag: float32 [8192], P('col')
- input_factor_gradient: float32 [16, 8192], P(None, 'row')
- grad_b: float32 [16, 8192], P(None, 'col')
Inputs may be any that keep to these rules, and one draw needn't show every extreme that they name: `sequence_lengths`: each group's 8 lengths sum to 1024, and one of them is exactly 512.
All inputs are finite; a program needn't handle non-finite values.
Results may differ from a plain program's by a relative error of at most 0.0052.
Values may be sent and summed in bfloat16 or wider, within the bound.
A program may use at most 64 MiB of HBM per device.

v0:
```python
import jax
import jax.numpy as jnp
from jax import lax
from jax.sharding import Mesh
from jax.sharding import PartitionSpec as P

COL = ("col_0", "col_1")
ROW_COL = ("row", "col_0", "col_1")
DP_COL = ("dp", "col_0", "col_1")


norm_eps = 1e-06
highest_precision = lax.Precision.HIGHEST


def sent_to_all(shard, axis):
    copies = jnp.broadcast_to(shard, (lax.axis_size(axis), *shard.shape))
    return lax.all_to_all(copies, axis, split_axis=0, concat_axis=0, tiled=True)


def laid_out(blocks, dim):
    blocks = jnp.moveaxis(blocks, 0, dim)
    shape = blocks.shape
    return blocks.reshape(*shape[:dim], shape[dim] * shape[dim + 1], *shape[dim + 2 :])


def gather_axes(shard, axes, dim):
    far, near = axes
    initial = sent_to_all(shard, far)
    blocks = jnp.swapaxes(sent_to_all(initial, near), 0, 1)
    return laid_out(blocks.reshape(-1, *shard.shape), dim)


def cut_along(shard, dim, size):
    shape = shard.shape
    blocks = shard.reshape(*shape[:dim], size, shape[dim] // size, *shape[dim + 1 :])
    return jnp.moveaxis(blocks, dim, 0)


def sum_at_owner(shard, axis, dim):
    size = lax.axis_size(axis)
    blocks = lax.all_to_all(cut_along(shard, dim, size), axis, 0, 0, tiled=True)
    return jnp.sum(blocks, axis=0)


def side_by_side(arrays, axis, dim, along):
    widths = [a.shape[along] for a in arrays]
    both = jnp.concatenate(arrays, axis=along)
    filled = sum_at_owner(both, axis, dim)
    return tuple(jnp.split(filled, [sum(widths[:k]) for k in range(1, len(widths))], axis=along))


def over_copies(shard, axis):
    everything = sent_to_all(shard, axis)
    return jnp.sum(everything, axis=0)


def together(arrays, axis):
    ravelled, at, outs = (jnp.concatenate([a.reshape(-1) for a in arrays]), 0, [])
    total = over_copies(ravelled, axis)
    for a in arrays:
        outs.append(total[at : at + a.size].reshape(a.shape))
        at += a.size
    return tuple(outs)


def rows_for(lines, size):
    spare = -len(lines) % size
    return jnp.pad(lines, [(0, spare)] + [(0, 0)] * (lines.ndim - 1))


def collect(shard, axis, dim):
    blocks = sent_to_all(shard, axis)
    return laid_out(blocks, dim)


def total_of(shard, axes):
    lines = shard.reshape(-1, shard.shape[-1])
    own = sum_at_owner(rows_for(lines, lax.axis_size(axes)), axes, 0)
    whole = collect(own, axes, 0)
    return whole[: len(lines)].reshape(shard.shape)


def sum_by_axis(shard, axes, dim):
    far, near = axes
    blocks = cut_along(shard, dim, lax.axis_size(far))
    nearer = sum_at_owner(blocks, near, dim + 1)
    arrived = lax.all_to_all(nearer, far, split_axis=0, concat_axis=0, tiled=True)
    return arrived.sum(axis=0)


def total_of_2(shard, axes):
    lines = shard.reshape(-1)
    padded = rows_for(lines, lax.axis_size(axes[0]) * lax.axis_size(axes[1]))
    whole = gather_axes(sum_by_axis(padded, axes, 0), axes, 0)
    return lax.slice_in_dim(whole, 0, len(lines)).reshape(shard.shape)


def contract_product(left, right, left_dim, right_dim):
    return lax.dot_general(
        left, right, (((left_dim,), (right_dim,)), ((), ())), preferred_element_type=jnp.float32
    )


def per_device(
    tokens,
    frozen_weight,
    input_adapter_factor,
    output_adapter_factor,
    magnitude,
    cotangent,
    sequence_lengths,
):
    row_count = lax.axis_size("row")
    col_count = lax.axis_size(COL)
    row_index = lax.axis_index("row")
    col_index = lax.axis_index(COL)
    group_index = lax.axis_index("dp")
    local_rows = tokens.shape[0]
    group_rows = local_rows * col_count
    block_rows = group_rows // row_count
    adapter_rank_size = input_adapter_factor.shape[0]
    low_rank_update = contract_product(input_adapter_factor, output_adapter_factor, 0, 0)
    merged = frozen_weight.astype(jnp.float32) + low_rank_update
    norm_terms = jnp.sum(merged * merged, axis=0)
    gram_partial_terms = contract_product(input_adapter_factor, input_adapter_factor, 1, 1)
    merged_factor_terms = jnp.dot(
        input_adapter_factor, frozen_weight, preferred_element_type=jnp.float32
    ) + jnp.dot(
        gram_partial_terms, output_adapter_factor.astype(jnp.float32), precision=highest_precision
    )
    portion = gather_axes(tokens, ("col_0", "col_1"), 0)
    base_piece = jnp.dot(portion, frozen_weight, preferred_element_type=jnp.float32)
    down_portion = contract_product(portion, input_adapter_factor, 1, 1)
    frozen_rows, down_rows = side_by_side((base_piece, down_portion), "row", 0, 1)
    norm_sq, merged_input_factor = together((norm_terms, merged_factor_terms), "row")
    down_activations = down_rows.astype(jnp.bfloat16)
    col_norm = jnp.sqrt(norm_sq + norm_eps)
    col_scale = magnitude / col_norm
    query_projection = frozen_rows + jnp.dot(
        down_activations, output_adapter_factor, preferred_element_type=jnp.float32
    )
    projected = (query_projection * col_scale[None, :]).astype(jnp.bfloat16)
    lengths = sequence_lengths[0]
    ends = jnp.cumsum(lengths, dtype=jnp.int32)
    starts = ends - lengths
    positions = row_index * block_rows + jnp.arange(block_rows, dtype=jnp.int32)
    inside = (positions[:, None] >= starts[None, :]) & (positions[:, None] < ends[None, :])
    inverse = 1.0 / lengths.astype(jnp.float32)
    weights = jnp.sum(jnp.where(inside, inverse[None, :], jnp.float32(0.0)), axis=1)
    grad_out = cotangent.astype(jnp.float32) * weights[:, None]
    scale_terms = jnp.sum(grad_out * query_projection, axis=0)
    projection_gradient = (grad_out * col_scale[None, :]).astype(jnp.bfloat16)
    bgrad_terms = contract_product(down_activations, projection_gradient, 0, 0)
    scale_grad, bgrad_data = together((scale_terms, bgrad_terms), ("dp", "row"))
    grad_mag = scale_grad / col_norm
    norm_coefficient = -scale_grad * magnitude / (col_norm * col_norm * col_norm)
    grad_b = bgrad_data + merged_input_factor * norm_coefficient[None, :]
    backward_terms = contract_product(projection_gradient, output_adapter_factor, 1, 1)
    padded = lax.dynamic_update_slice_in_dim(
        jnp.zeros((group_rows, adapter_rank_size), jnp.float32),
        backward_terms,
        row_index * block_rows,
        0,
    )
    backward_rows = total_of(padded, ROW_COL).astype(jnp.bfloat16)
    back_mine = lax.dynamic_slice_in_dim(backward_rows, col_index * local_rows, local_rows, 0)
    row_term = contract_product(back_mine, tokens, 0, 0)
    scaled_output_factor = (
        output_adapter_factor.astype(jnp.float32) * norm_coefficient[None, :]
    ).astype(jnp.bfloat16)
    norm_term = contract_product(scaled_output_factor, frozen_weight, 1, 1) + jnp.dot(
        contract_product(scaled_output_factor, output_adapter_factor, 1, 1),
        input_adapter_factor.astype(jnp.float32),
        precision=highest_precision,
    )
    first_group = (group_index == 0).astype(jnp.float32)
    input_factor_gradient = total_of_2(
        row_term + first_group * norm_term, (("dp", "col_0"), "col_1")
    )
    return (projected, grad_mag, input_factor_gradient, grad_b)


def solution(mesh):
    split = Mesh(
        mesh.devices.reshape(mesh.shape["dp"], mesh.shape["row"], 8, 2),
        ("dp", "row", "col_0", "col_1"),
    )
    return jax.shard_map(
        per_device,
        mesh=split,
        in_specs=(
            P(DP_COL, "row"),
            P("row", COL),
            P(None, "row"),
            P(None, COL),
            P(COL),
            P(("dp", "row"), COL),
            P("dp", None),
        ),
        out_specs=(P(("dp", "row"), COL), P(COL), P(None, "row"), P(None, COL)),
        check_vma=False,
    )
```

profile of v0, /device:TPU:1, one launch (start us, length us, event | category | flops | bytes accessed | tf_op | source)
XLA Modules:
  0.0 235.9 jit_solution(9612073964963525461)
XLA Ops:
  0.7 0.8 copy-done
  1.5 0.1 fusion.17
  1.6 2.0 fusion.16
  3.6 0.7 multiply_reduce_fusion
  4.4 0.1 fusion.2
  4.6 9.5 %all_to_all.65 = f32[4,1,8704]{2,1,0:T(1,128)S(1)} all-to-all(f32[4,1,8704]{2,1,0:T(1,128)S(1)} %broadcast_in_dim.50), channel_id=1, replica_groups=mesh['dp'=8,'row'=4,'col_0'=8,'col_1'=2] {'row'}, dimensions={0} | all-to-all | bytes 278528 | tf_op jit(solution)/shard_map/all_to_all | solution.py:18
  14.1 1.6 broadcast_in_dim.48
  15.7 10.2 %all-to-all-start = ((bf16[8,64,2048]{2,1,0:T(8,128)(2,1)}), bf16[8,64,2048]{2,1,0:T(8,128)(2,1)S(1)}, u32[]{:S(2)}, u32[]{:S(2)}) async-start(bf16[8,64,2048]{2,1,0:T(8,128)(2,1)} %broadcast_in_dim.48), calls=%async_computation | async-start | bytes 4194304 | tf_op jit(solution)/shard_map/all_to_all | solution.py:18
  25.9 0.2 reduce-window.4
  26.1 0.1 select_reduce_fusion
  26.2 0.1 reduce_sum.83
  26.4 0.6 copy-done.9
  27.0 0.2 convolution_dynamic-update-slice_fusion
  27.2 0.2 reshape.78
  27.4 0.3 copy.68
  27.8 0.9 reshape.79
  28.6 49.0 %all-to-all-done = bf16[8,64,2048]{2,1,0:T(8,128)(2,1)S(1)} async-done(((bf16[8,64,2048]{2,1,0:T(8,128)(2,1)}), bf16[8,64,2048]{2,1,0:T(8,128)(2,1)S(1)}, u32[]{:S(2)}, u32[]{:S(2)}) %all-to-all-start) | async-done | bytes 2097184 | tf_op jit(solution)/shard_map/all_to_all | solution.py:18
  77.6 0.5 broadcast_in_dim.49
  78.1 8.3 %all_to_all.66 = bf16[2,8,64,2048]{3,2,1,0:T(8,128)(2,1)} all-to-all(bf16[2,8,64,2048]{3,2,1,0:T(8,128)(2,1)S(1)} %broadcast_in_dim.49), channel_id=1, replica_groups=mesh['dp'=8,'row'=4,'col_0'=8,'col_1'=2] {'col_1'}, dimensions={0} | all-to-all | bytes 8388608 | tf_op jit(solution)/shard_map/all_to_all | solution.py:18
  86.4 4.4 %all-to-all-start.5 = ((f32[64,1,256]{2,1,0:T(1,128)}), f32[64,1,256]{2,1,0:T(1,128)S(1)}, u32[]{:S(2)}, u32[]{:S(2)}) async-start(f32[64,1,256]{2,1,0:T(1,128)} %reshape.79), calls=%async_computation.5 | async-start | bytes 131072 | tf_op jit(solution)/shard_map/all_to_all | solution.py:42
  90.9 2.5 %copy.37 = bf16[2,8,64,2048]{3,2,0,1:T(8,128)(2,1)S(1)} copy(bf16[2,8,64,2048]{3,2,1,0:T(8,128)(2,1)} %all_to_all.66) | data formatting | bytes 8388608 | tf_op jit(solution)/shard_map/all_to_all | solution.py:18
  93.4 1.2 fusion.15
  94.6 0.4 copy-done.2
  95.0 2.4 %fusion.14 = f32[1024,512]{0,1:T(8,128)S(1)} fusion(bf16[1024,2048]{1,0:T(8,128)(2,1)S(1)} %bitcast.58, bf16[2048,512]{1,0:T(8,128)(2,1)S(1)} %copy-done.2), kind=kOutput, calls=%fused_computation.42 | convolution fusion | flops 2147483648 | bytes 8388608 | tf_op jit(solution)/shard_map/dot_general | solution.py:133
  97.4 0.2 pad_maximum_fusion
  97.7 1.5 copy.65
  99.2 1.6 all-to-all-done.5
  100.7 3.6 %all-to-all-start.2 = ((f32[4,256,528]{1,2,0:T(8,128)}), f32[4,256,528]{1,2,0:T(8,128)S(1)}, u32[]{:S(2)}, u32[]{:S(2)}) async-start(f32[4,256,528]{1,2,0:T(8,128)} %bitcast.59), calls=%async_computation.2 | async-start | bytes 4325376 | tf_op jit(solution)/shard_map/all_to_all | solution.py:42
  104.4 0.5 broadcast.22
  104.9 0.8 reduce.3
  105.7 0.2 reshape.80
  105.9 0.1 bitcast_reduce_fusion
  106.0 0.1 copy.45
  106.1 0.8 reshape.81
  106.9 24.2 %all-to-all-done.2 = f32[4,256,528]{1,2,0:T(8,128)S(1)} async-done(((f32[4,256,528]{1,2,0:T(8,128)}), f32[4,256,528]{1,2,0:T(8,128)S(1)}, u32[]{:S(2)}, u32[]{:S(2)}) %all-to-all-start.2) | async-done | bytes 2162720 | tf_op jit(solution)/shard_map/all_to_all | solution.py:42
  131.1 8.3 %all-to-all-start.6 = ((bf16[64,2,128]{2,1,0:T(2,128)(2,1)}), bf16[64,2,128]{2,1,0:T(2,128)(2,1)S(1)}, u32[]{:S(2)}, u32[]{:S(2)}) async-start(bf16[64,2,128]{2,1,0:T(2,128)(2,1)} %reshape.81), calls=%async_computation.6 | async-start | bytes 65536 | tf_op jit(solution)/shard_map/all_to_all | solution.py:18
  139.4 0.2 reduce_sum.81
  139.6 0.2 convolution_bitcast_fusion
  139.9 0.2 copy.53
  140.1 1.0 multiply_reduce_fusion.1
  141.1 7.6 %all-to-all-done.6 = bf16[64,2,128]{2,1,0:T(2,128)(2,1)S(1)} async-done(((bf16[64,2,128]{2,1,0:T(2,128)(2,1)}), bf16[64,2,128]{2,1,0:T(2,128)(2,1)S(1)}, u32[]{:S(2)}, u32[]{:S(2)}) %all-to-all-start.6) | async-done | bytes 32800 | tf_op jit(solution)/shard_map/all_to_all | solution.py:18
  148.6 1.6 broadcast_in_dim.54
  150.2 8.3 %all-to-all-start.4 = ((f32[32,1,8704]{2,1,0:T(1,128)}), f32[32,1,8704]{2,1,0:T(1,128)S(1)}, u32[]{:S(2)}, u32[]{:S(2)}) async-start(f32[32,1,8704]{2,1,0:T(1,128)} %broadcast_in_dim.54), calls=%async_computation.4 | async-start | bytes 2228224 | tf_op jit(solution)/shard_map/all_to_all | solution.py:18
  158.6 1.7 reshape.82
  160.2 1.6 fusion.7
  161.8 24.0 %all-to-all-done.4 = f32[32,1,8704]{2,1,0:T(1,128)S(1)} async-done(((f32[32,1,8704]{2,1,0:T(1,128)}), f32[32,1,8704]{2,1,0:T(1,128)S(1)}, u32[]{:S(2)}, u32[]{:S(2)}) %all-to-all-start.4) | async-done | bytes 1114144 | tf_op jit(solution)/shard_map/all_to_all | solution.py:18
  185.8 0.6 reduce_sum.86
  186.4 1.3 fusion.9
  187.8 0.6 fusion.4
  188.4 0.1 fusion.3
  188.6 0.2 fusion.1
  188.8 0.1 reshape_reshape.7
  188.9 6.4 %all_to_all.67 = f32[2,64,256]{2,1,0:T(8,128)S(1)} all-to-all(f32[2,64,256]{2,1,0:T(8,128)S(1)} %bitcast.62), channel_id=1, replica_groups=mesh['dp'=8,'row'=4,'col_0'=8,'col_1'=2] {'col_1'}, dimensions={0} | all-to-all | bytes 262144 | tf_op jit(solution)/shard_map/all_to_all | solution.py:42
  195.4 0.7 all_to_all.49
  196.1 4.9 %all-to-all-start.8 = ((f32[64,1,256]{2,1,0:T(1,128)}), f32[64,1,256]{2,1,0:T(1,128)S(1)}, u32[]{:S(2)}, u32[]{:S(2)}) async-start(f32[64,1,256]{2,1,0:T(1,128)} %all_to_all.49), calls=%async_computation.8 | async-start | bytes 131072 | tf_op jit(solution)/shard_map/all_to_all | solution.py:88
  201.1 11.1 %all-to-all-done.8 = f32[64,1,256]{2,1,0:T(1,128)S(1)} async-done(((f32[64,1,256]{2,1,0:T(1,128)}), f32[64,1,256]{2,1,0:T(1,128)S(1)}, u32[]{:S(2)}, u32[]{:S(2)}) %all-to-all-start.8) | async-done | bytes 65568 | tf_op jit(solution)/shard_map/all_to_all | solution.py:88
  212.1 0.1 reduce_sum.89
  212.2 0.7 broadcast_in_dim.57
  212.9 4.6 %all-to-all-start.9 = ((f32[64,1,256]{2,1,0:T(1,128)}), f32[64,1,256]{2,1,0:T(1,128)S(1)}, u32[]{:S(2)}, u32[]{:S(2)}) async-start(f32[64,1,256]{2,1,0:T(1,128)} %broadcast_in_dim.57), calls=%async_computation.9 | async-start | bytes 131072 | tf_op jit(solution)/shard_map/all_to_all | solution.py:18
  217.5 0.6 multiply_add_fusion
  218.2 10.5 %all-to-all-done.9 = f32[64,1,256]{2,1,0:T(1,128)S(1)} async-done(((f32[64,1,256]{2,1,0:T(1,128)}), f32[64,1,256]{2,1,0:T(1,128)S(1)}, u32[]{:S(2)}, u32[]{:S(2)}) %all-to-all-start.9) | async-done | bytes 65568 | tf_op jit(solution)/shard_map/all_to_all | solution.py:18
  228.6 6.4 %all_to_all.68 = f32[2,64,256]{2,1,0:T(8,128)S(1)} all-to-all(f32[2,64,256]{2,1,0:T(8,128)S(1)} %broadcast_in_dim.58), channel_id=1, replica_groups=mesh['dp'=8,'row'=4,'col_0'=8,'col_1'=2] {'col_1'}, dimensions={0} | all-to-all | bytes 262144 | tf_op jit(solution)/shard_map/all_to_all | solution.py:18
  235.0 0.1 copy.47
  235.1 0.8 reshape_reshape_reshape.3
  (45 shorter events, 0.3 us)
Async XLA Ops:
  0.6 0.8 copy-start
  0.6 2.9 %copy-start.1 = (bf16[2048,512]{1,0:T(8,128)(2,1)S(1)}, bf16[2048,512]{1,0:T(8,128)(2,1)}, u32[]{:S(2)}) copy-start(bf16[2048,512]{1,0:T(8,128)(2,1)} %param.8) | copy-start | bytes 6291460
  0.7 2.9 %copy-start.6 = (bf16[16,512]{1,0:T(8,128)(2,1)S(1)}, bf16[16,512]{1,0:T(8,128)(2,1)}, u32[]{:S(2)}) copy-start(bf16[16,512]{1,0:T(8,128)(2,1)} %param.10) | copy-start | bytes 49156
  3.6 10.5 %copy-start.4 = (bf16[64,2048]{1,0:T(8,128)(2,1)S(1)}, bf16[64,2048]{1,0:T(8,128)(2,1)}, u32[]{:S(2)}) copy-start(bf16[64,2048]{1,0:T(8,128)(2,1)} %param.7) | copy-start | bytes 786436
  15.7 10.2 %copy-start.13 = (s32[1,8]{1,0:T(1,128)S(1)}, s32[1,8]{1,0:T(1,128)}, u32[]{:S(2)}) copy-start(s32[1,8]{1,0:T(1,128)} %param.13) | copy-start | bytes 100
  15.7 10.6 %copy-start.12 = (f32[512]{0:T(512)S(1)}, f32[512]{0:T(512)}, u32[]{:S(2)}) copy-start(f32[512]{0:T(512)} %param.11) | copy-start | bytes 6148
  15.7 11.2 %copy-start.7 = (bf16[256,512]{1,0:T(8,128)(2,1)S(1)}, bf16[256,512]{1,0:T(8,128)(2,1)}, u32[]{:S(2)}) copy-start(bf16[256,512]{1,0:T(8,128)(2,1)} %param.12) | copy-start | bytes 786436
  15.7 61.8 %all-to-all-start = ((bf16[8,64,2048]{2,1,0:T(8,128)(2,1)}), bf16[8,64,2048]{2,1,0:T(8,128)(2,1)S(1)}, u32[]{:S(2)}, u32[]{:S(2)}) async-start(bf16[8,64,2048]{2,1,0:T(8,128)(2,1)} %broadcast_in_dim.48), calls=%async_computation | async-start | bytes 4194304 | tf_op jit(solution)/shard_map/all_to_all | solution.py:18
  26.4 0.6 copy-start.9
  86.4 14.3 %all-to-all-start.5 = ((f32[64,1,256]{2,1,0:T(1,128)}), f32[64,1,256]{2,1,0:T(1,128)S(1)}, u32[]{:S(2)}, u32[]{:S(2)}) async-start(f32[64,1,256]{2,1,0:T(1,128)} %reshape.79), calls=%async_computation.5 | async-start | bytes 131072 | tf_op jit(solution)/shard_map/all_to_all | solution.py:42
  93.4 1.6 copy-start.2
  100.7 30.3 %all-to-all-start.2 = ((f32[4,256,528]{1,2,0:T(8,128)}), f32[4,256,528]{1,2,0:T(8,128)S(1)}, u32[]{:S(2)}, u32[]{:S(2)}) async-start(f32[4,256,528]{1,2,0:T(8,128)} %bitcast.59), calls=%async_computation.2 | async-start | bytes 4325376 | tf_op jit(solution)/shard_map/all_to_all | solution.py:42
  106.1 33.5 %copy-start.8 = (bf16[256,512]{1,0:T(8,128)(2,1)S(1)}, bf16[256,512]{1,0:T(8,128)(2,1)}, u32[]{:S(2)}) copy-start(bf16[256,512]{1,0:T(8,128)(2,1)} %param.12) | copy-start | bytes 786436
  131.1 17.5 %all-to-all-start.6 = ((bf16[64,2,128]{2,1,0:T(2,128)(2,1)}), bf16[64,2,128]{2,1,0:T(2,128)(2,1)S(1)}, u32[]{:S(2)}, u32[]{:S(2)}) async-start(bf16[64,2,128]{2,1,0:T(2,128)(2,1)} %reshape.81), calls=%async_computation.6 | async-start | bytes 65536 | tf_op jit(solution)/shard_map/all_to_all | solution.py:18
  148.6 1.6 copy-start.11
  150.2 37.6 %copy-start.3 = (bf16[2048,512]{1,0:T(8,128)(2,1)S(1)}, bf16[2048,512]{1,0:T(8,128)(2,1)}, u32[]{:S(2)}) copy-start(bf16[2048,512]{1,0:T(8,128)(2,1)} %param.8) | copy-start | bytes 6291460
  150.2 35.6 %all-to-all-start.4 = ((f32[32,1,8704]{2,1,0:T(1,128)}), f32[32,1,8704]{2,1,0:T(1,128)S(1)}, u32[]{:S(2)}, u32[]{:S(2)}) async-start(f32[32,1,8704]{2,1,0:T(1,128)} %broadcast_in_dim.54), calls=%async_computation.4 | async-start | bytes 2228224 | tf_op jit(solution)/shard_map/all_to_all | solution.py:18
  161.8 26.8 %copy-start.5 = (f32[16,2048]{1,0:T(8,128)S(1)}, f32[16,2048]{1,0:T(8,128)}, u32[]{:S(2)}) copy-start(f32[16,2048]{1,0:T(8,128)} %fusion.7) | copy-start | bytes 393220
  186.4 14.6 %copy-start.10 = (f32[8704]{0:T(1024)S(1)}, f32[8704]{0:T(1024)}, u32[]{:S(2)}) copy-start(f32[8704]{0:T(1024)} %copy-done.9) | copy-start | bytes 104452
  196.1 16.1 %all-to-all-start.8 = ((f32[64,1,256]{2,1,0:T(1,128)}), f32[64,1,256]{2,1,0:T(1,128)S(1)}, u32[]{:S(2)}, u32[]{:S(2)}) async-start(f32[64,1,256]{2,1,0:T(1,128)} %all_to_all.49), calls=%async_computation.8 | async-start | bytes 131072 | tf_op jit(solution)/shard_map/all_to_all | solution.py:88
  212.9 15.7 %all-to-all-start.9 = ((f32[64,1,256]{2,1,0:T(1,128)}), f32[64,1,256]{2,1,0:T(1,128)S(1)}, u32[]{:S(2)}, u32[]{:S(2)}) async-start(f32[64,1,256]{2,1,0:T(1,128)} %broadcast_in_dim.57), calls=%async_computation.9 | async-start | bytes 131072 | tf_op jit(solution)/shard_map/all_to_all | solution.py:18
where the time goes:
time: 237 us; the launch traced here: 236 us
  waiting for transfers between devices  128 us (54%)
  starting transfers between devices  44.4 us (19%)
  blocking collectives  30.7 us (13%)
  local copies, waits for them, and re-layouts  16.9 us (7%)
  matrix products  10.6 us (4%)
  other arithmetic  4.45 us (2%)
    all_to_all x4, waiting for transfers between devices, sent_to_all(): return lax.all_to_all(copies, axis, split_axis=0, concat_axis=0, tiled=True)  91 us
    all_to_all x4, starting transfers between devices, sent_to_all(): return lax.all_to_all(copies, axis, split_axis=0, concat_axis=0, tiled=True)  31.4 us
    all_to_all x2, waiting for transfers between devices, sum_at_owner(): blocks = lax.all_to_all(cut_along(shard, dim, size), axis, 0, 0, tiled=True)  25.7 us
    all_to_all x3, blocking collectives, sent_to_all(): return lax.all_to_all(copies, axis, split_axis=0, concat_axis=0, tiled=True)  24.2 us
    all_to_all x1, waiting for transfers between devices, sum_by_axis(): lax.all_to_all(nearer, far, split_axis=0, concat_axis=0, tiled=True)  11.1 us
    all_to_all x2, starting transfers between devices, sum_at_owner(): blocks = lax.all_to_all(cut_along(shard, dim, size), axis, 0, 0, tiled=True)  8.04 us
    all_to_all x1, blocking collectives, sum_at_owner(): blocks = lax.all_to_all(cut_along(shard, dim, size), axis, 0, 0, tiled=True)  6.45 us
    unnamed x36, local copies, waits for them, and re-layouts  5.58 us
  transfers between devices with their start and end apart: 7, of which 7 were waited for; matrix products, arithmetic and copies ran while one was open for 8% of the time, Pallas kernels for 0%

commit v1 on v0

v1 whole, which is shorter than its diff:
```python
import functools

import jax
import jax.numpy as jnp
from jax import lax
from jax.experimental import pallas as pl
from jax.experimental.pallas import tpu as pltpu
from jax.sharding import Mesh
from jax.sharding import PartitionSpec as P

AXES = ("dp", "row", "z", "core")
COL = ("z", "core")
EPS = 1e-06
F32 = jnp.float32
BF16 = jnp.bfloat16
HIGHEST = lax.Precision.HIGHEST


def nn(a, b):
    return lax.dot_general(a, b, (((1,), (0,)), ((), ())), preferred_element_type=F32)


def nt(a, b):
    return lax.dot_general(a, b, (((1,), (1,)), ((), ())), preferred_element_type=F32)


def tn(a, b):
    return lax.dot_general(a, b, (((0,), (0,)), ((), ())), preferred_element_type=F32)


def exact(a, b):
    return lax.dot_general(
        a, b, (((1,), (0,)), ((), ())), preferred_element_type=F32, precision=HIGHEST
    )


def fold(a):
    return jnp.sum(a.reshape(a.shape[0] // 8, 8, a.shape[1]), axis=0)


def kernel(
    sizes,
    tok_hbm, w_hbm, a_hbm, b_hbm, mag_ref, ct_hbm, lens_ref,
    proj_ref, gmag_ref, ifg_ref, gb_ref,
    T, W, A, B, CT, WT, PF, PS, PR, DB,
    NX, AX, SACC, SX, SY, SCALE, NORM, BG, BGS, BX, BY, R, RY, H, CX, ZX, AM,
    load_sem, zr_s, zr_r, zl_s, zl_r, dr_s, dr_r, dl_s, dl_r, do_s, do_r,
    ct_s, ct_r, p_s, p_r, nx_s, nx_r, ax_s, ax_r, sx_s, sx_r, sy_s, sy_r,
    bx_s, bx_r, by_s, by_r, bo_s, bo_r, ry_s, ry_r, cx_s, cx_r, zx_s, zx_r,
    yo_s, yo_r, co_s, co_r,
):
    ny, nx, nz = sizes
    y, x, z, k = (lax.axis_index(a) for a in AXES)
    rows = tok_hbm.shape[0]
    half = rows // 2
    unit = 2 * rows
    own = nz // nx * unit
    per = nz // nx
    slab = T.shape[1] // ny
    lane = slab // 2
    part = W.shape[1] // nx

    def at(axis, index):
        return tuple(index if i == axis else v for i, v in enumerate((y, x, z, k)))

    def step(axis, by, n):
        return at(axis, lax.rem((y, x, z)[axis] + by + n, n))

    partner = (y, x, z, 1 - k)
    right = step(2, 1, nz)
    left = step(2, -1, nz)

    def copy(src, dst, ssem, rsem, dev):
        return pltpu.make_async_remote_copy(
            src_ref=src, dst_ref=dst, send_sem=ssem, recv_sem=rsem,
            device_id=dev, device_id_type=pl.DeviceIdType.MESH,
        )

    barrier = pltpu.get_barrier_semaphore()
    greeted = 0
    for axis, n in ((0, ny), (1, nx), (2, nz)):
        for d in range(1, n):
            pl.semaphore_signal(
                barrier, inc=1, device_id=step(axis, d, n), device_id_type=pl.DeviceIdType.MESH
            )
            greeted += 1
    pl.semaphore_signal(barrier, inc=1, device_id=partner, device_id_type=pl.DeviceIdType.MESH)
    greeted += 1

    def token_rows(chip, core, h, n):
        return pl.ds(pl.multiple_of(chip * unit + core * rows + h * half, half), n)

    mine = token_rows(z, k, 0, rows)
    owned = pl.ds(pl.multiple_of(x * own, own), own)
    loads = [
        pltpu.make_async_copy(tok_hbm, T.at[mine], load_sem.at[0]),
        pltpu.make_async_copy(ct_hbm, CT.at[owned], load_sem.at[1]),
        pltpu.make_async_copy(a_hbm, A, load_sem.at[2]),
        pltpu.make_async_copy(b_hbm, B, load_sem.at[3]),
        pltpu.make_async_copy(w_hbm, W, load_sem.at[4]),
    ]
    for c in loads:
        c.start()

    seqs = lens_ref.shape[1]

    def weigh(i, _):
        pos = lax.broadcasted_iota(jnp.int32, (unit, 128), 0) + i * unit
        total = jnp.zeros((unit, 128), F32)
        start = jnp.int32(0)
        for s in range(seqs):
            length = lens_ref[0, s]
            end = start + length
            inverse = 1.0 / jnp.full((1, 128), length, jnp.int32).astype(F32)
            total += jnp.where((pos >= start) & (pos < end), inverse, 0.0)
            start = end
        WT[pl.ds(pl.multiple_of(i * unit, unit), unit), :] = total
        return 0

    lax.fori_loop(0, nz, weigh, 0)

    loads[0].wait()
    loads[1].wait()
    pl.semaphore_wait(barrier, greeted)

    def ring(right_way, src_chip, h, idx):
        r = token_rows(src_chip, k, h, half)
        if right_way:
            return copy(T.at[r], T.at[r], zr_s.at[idx], zr_r.at[idx], right)
        return copy(T.at[r], T.at[r], zl_s.at[idx], zl_r.at[idx], left)

    def across(right_way, src_chip, core, h, idx):
        r = token_rows(src_chip, core, h, half)
        if right_way:
            return copy(T.at[r], T.at[r], dr_s.at[idx], dr_r.at[idx], partner)
        return copy(T.at[r], T.at[r], dl_s.at[idx], dl_r.at[idx], partner)

    def across_own(core):
        r = token_rows(z, core, 0, rows)
        return copy(T.at[r], T.at[r], do_s.at[0], do_r.at[0], partner)

    steps = nz // 2
    last = 2 * steps - 2
    ring(True, z, 0, 0).start()
    ring(False, z, 0, 0).start()
    ring(True, z, 1, 1).start()
    ring(False, z, 1, 1).start()
    across_own(k).start()

    def chip_of(j):
        s = (j + 1) // 2
        return lax.rem(z + nz + jnp.where(lax.rem(j, 2) == 1, -s, s), nz)

    def unit_rows(chip):
        return pl.ds(pl.multiple_of(chip * unit, unit), unit)

    def ct_copy(chip, d):
        r = unit_rows(chip)
        return copy(
            CT.at[r], CT.at[r], ct_s.at[(d - 1) * per + lax.rem(chip, per)], ct_r.at[chip],
            step(1, d, nx),
        )

    def send_ct(j, _):
        chip = chip_of(j)

        @pl.when(chip // per == x)
        def _():
            for d in range(1, nx):
                ct_copy(chip, d).start()

        return 0

    for c in loads[2:]:
        c.wait()
    chunk = slab

    def norm_part(i, acc):
        c = pl.ds(pl.multiple_of(i * chunk, chunk), chunk)
        m = W[c, :].astype(F32) + tn(A[:, c], B[...])
        return acc + fold(m * m)

    acc = lax.fori_loop(0, ny, norm_part, jnp.zeros((8, W.shape[1]), F32))
    NX[x] = jnp.sum(acc, axis=0, keepdims=True)

    def to_x(src, slot, ssem, rsem, d):
        return copy(src, slot, ssem.at[d - 1], rsem.at[x], step(1, d, nx))

    def from_x(slots, rsem, ssem, d):
        src = lax.rem(x + d, nx)
        return copy(slots.at[src], slots.at[src], ssem.at[d - 1], rsem.at[src], step(1, d, nx))

    for d in range(1, nx):
        to_x(NX.at[x], NX.at[x], nx_s, nx_r, d).start()
    lax.fori_loop(0, nz, send_ct, 0)

    am = nn(A[...], W[...]) + exact(nt(A[...], A[...]), B[...].astype(F32))
    for i in range(nx):
        AM[i] = am[:, i * part : (i + 1) * part]

    SACC[...] = jnp.zeros_like(SACC)
    BG[...] = jnp.zeros_like(BG)
    R[...] = jnp.zeros_like(R)

    for d in range(1, nx):
        dst = lax.rem(x + d, nx)
        copy(AM.at[dst], AX.at[x], ax_s.at[d - 1], ax_r.at[x], step(1, d, nx)).start()
    AX[x] = AM[x]

    def project(chip):
        r = unit_rows(chip)
        t = T[r, :]
        down = nt(t, A[...]).astype(BF16)
        p = nn(t, W[...]) + nn(down, B[...])
        DB[r, :] = down
        PF[r, :] = p
        PS[r, :] = p.astype(BF16)

    def need_ct(chip):
        @pl.when(chip // per != x)
        def _():
            ct_copy(chip, 1).wait_recv()

    def weighted(chip):
        r = unit_rows(chip)
        w = WT[r, :]
        return CT[r, :].astype(F32) * jnp.concatenate([w] * (W.shape[1] // 128), axis=1)

    def scale_sum(chip):
        SACC[...] += fold(weighted(chip) * PF[unit_rows(chip), :])

    def backward(chip):
        r = unit_rows(chip)
        gp = (weighted(chip) * SCALE[...]).astype(BF16)
        BG[...] += tn(DB[r, :], gp)
        back = nt(B[...], gp)
        high = back.astype(BF16)
        low = (back - high.astype(F32)).astype(BF16)
        both = nn(jnp.concatenate([high, low], axis=0), T[r, :])
        R[...] += both[: back.shape[0]] + both[back.shape[0] :]

    def p_copy(chip, src, dst):
        loc = lax.rem(chip, per)
        r = pl.ds(pl.multiple_of(loc * unit, unit), unit)
        return copy(
            PS.at[unit_rows(chip)], PR.at[src, r], p_s.at[chip], p_r.at[src * per + loc], at(1, dst)
        )

    def send_p(chip):
        @pl.when(chip // per != x)
        def _():
            p_copy(chip, x, chip // per).start()

    def handle(i):
        s = i // 2 + 1
        h = lax.rem(i, 2)
        hr = h
        hl = jnp.where(i == last, 1, h)
        fr = lax.rem(z - s + nz, nz)
        fl = lax.rem(z + s, nz)
        ring(True, fr, hr, i).wait_recv()

        @pl.when(i < last - 1)
        def _():
            ring(True, fr, hr, i + 2).start()

        across(True, fr, k, hr, i).start()
        ring(False, fl, hl, i).wait_recv()

        @pl.when((i < last - 2) | (i == last - 1))
        def _():
            ring(False, fl, hl, jnp.where(i == last - 1, last, i + 2)).start()

        across(False, fl, k, hl, i).start()

    def need_tokens(j):
        @pl.when(j == 0)
        def _():
            across_own(1 - k).wait_recv()

        s = (j + 1) // 2

        @pl.when((lax.rem(j, 2) == 1) & (j < nz - 1))
        def _():
            for h in range(2):
                across(True, chip_of(j), 1 - k, h, j - 1 + h).wait_recv()

        @pl.when((lax.rem(j, 2) == 0) & (j > 0))
        def _():
            for h in range(2):
                across(False, chip_of(j), 1 - k, h, j - 2 + h).wait_recv()

        @pl.when(j == nz - 1)
        def _():
            across(True, chip_of(j), 1 - k, 0, last).wait_recv()
            across(False, chip_of(j), 1 - k, 1, last).wait_recv()

    lag = 2
    held = nz - 3

    def turn(j, _):
        chip = chip_of(j)
        need_tokens(j)
        project(chip)

        @pl.when(j == 1)
        def _():
            for d in range(1, nx):
                from_x(NX, nx_r, nx_s, d).wait_recv()
            sq = NX[0]
            for i in range(1, nx):
                sq = sq + NX[i]
            norm = jnp.sqrt(sq + EPS)
            NORM[...] = norm
            SCALE[...] = mag_ref[...] / norm

        @pl.when(j >= lag)
        def _():
            c = chip_of(j - lag)
            need_ct(c)
            scale_sum(c)
            backward(c)

        @pl.when(j == 0)
        def _():
            handle(0)

        @pl.when(j < nz - 3)
        def _():
            handle(j + 1)

        @pl.when(j == nz - 2)
        def _():
            handle(last)

        @pl.when(j < held)
        def _():
            send_p(chip)

        return 0

    lax.fori_loop(0, nz, turn, 0)

    def finish_s(j, _):
        c = chip_of(j)
        need_ct(c)
        scale_sum(c)
        return 0

    lax.fori_loop(nz - lag, nz, finish_s, 0)
    SX[x] = jnp.sum(SACC[...], axis=0, keepdims=True)
    for d in range(1, nx):
        to_x(SX.at[x], SX.at[x], sx_s, sx_r, d).start()

    def finish_b(j, _):
        backward(chip_of(j))
        return 0

    lax.fori_loop(nz - lag, nz, finish_b, 0)
    for i in range(ny):
        H[i] = R[:, i * slab : (i + 1) * slab]
    for i in range(nx):
        BGS[i] = BG[:, i * part : (i + 1) * part]

    for d in range(1, nx):
        from_x(SX, sx_r, sx_s, d).wait_recv()
    sx = SX[0]
    for i in range(1, nx):
        sx = sx + SX[i]
    SY[y] = sx

    def to_y(src, slot, ssem, rsem, d):
        return copy(src, slot, ssem.at[d - 1], rsem.at[y], step(0, d, ny))

    def from_y(slots, rsem, ssem, d):
        src = lax.rem(y + d, ny)
        return copy(slots.at[src], slots.at[src], ssem.at[d - 1], rsem.at[src], step(0, d, ny))

    for d in range(1, ny):
        to_y(SY.at[y], SY.at[y], sy_s, sy_r, d).start()
    for d in range(1, nx):
        dst = lax.rem(x + d, nx)
        copy(BGS.at[dst], BX.at[x], bx_s.at[d - 1], bx_r.at[x], step(1, d, nx)).start()
    BX[x] = BGS[x]
    for d in range(1, ny):
        dst = lax.rem(y + d, ny)
        copy(H.at[dst], RY.at[y], ry_s.at[d - 1], ry_r.at[y], step(0, d, ny)).start()
    RY[y] = H[y]

    def send_held(j, _):
        send_p(chip_of(j))
        return 0

    lax.fori_loop(held, nz, send_held, 0)

    for d in range(1, nx):
        from_x(BX, bx_r, bx_s, d).wait_recv()
    bx = BX[0]
    for i in range(1, nx):
        bx = bx + BX[i]
    BY[y] = bx
    for d in range(1, ny):
        to_y(BY.at[y], BY.at[y], by_s, by_r, d).start()

    for d in range(1, ny):
        from_y(SY, sy_r, sy_s, d).wait_recv()
    s_all = SY[0]
    for i in range(1, ny):
        s_all = s_all + SY[i]
    norm = NORM[...]
    gmag_ref[...] = s_all / norm
    coef = -s_all * mag_ref[...] / (norm * norm * norm)
    scaled = (B[...].astype(F32) * coef).astype(BF16)
    cols = pl.ds(pl.multiple_of(y * slab, slab), slab)
    part_y = nt(scaled, W[cols, :]) + exact(nt(scaled, B[...]), A[:, cols].astype(F32))
    for d in range(1, ny):
        from_y(RY, ry_r, ry_s, d).wait_recv()
    for i in range(ny):
        part_y = part_y + RY[i]

    CX[0] = part_y[:, :lane]
    CX[1] = part_y[:, lane:]
    cross = copy(CX.at[1 - k], CX.at[2], cx_s.at[0], cx_r.at[0], partner)
    cross.start()
    cross.wait_recv()
    ZX[z] = CX[k] + CX[2]

    def to_z(d):
        return copy(ZX.at[z], ZX.at[z], zx_s.at[d - 1], zx_r.at[z], step(2, d, nz))

    for d in range(1, nz):
        to_z(d).start()

    for d in range(1, ny):
        from_y(BY, by_r, by_s, d).wait_recv()
    b_all = BY[0]
    for i in range(1, ny):
        b_all = b_all + BY[i]
    for d in range(1, nx):
        from_x(AX, ax_r, ax_s, d).wait_recv()
    a_all = AX[0]
    for i in range(1, nx):
        a_all = a_all + AX[i]

    for i in range(nx):

        @pl.when(x == i)
        def _():
            c = slice(i * part, (i + 1) * part)
            gb_ref[:, c] = b_all + a_all * coef[:, c]

    def gb_part(i):
        return gb_ref.at[:, pl.ds(pl.multiple_of(i * part, part), part)]

    for d in range(1, nx):
        copy(gb_part(x), gb_part(x), bo_s.at[d - 1], bo_r.at[x], step(1, d, nx)).start()

    for d in range(1, nx):
        src = lax.rem(x + d, nx)
        for loc in range(per):
            p_copy(x * per + loc, src, src).wait_recv()
    rest = pl.ds(pl.multiple_of(x * own, own), own)
    total = PF[rest, :]
    for d in range(1, nx):
        total = total + PR[lax.rem(x + d, nx)].astype(F32)
    proj_ref[...] = (total * SCALE[...]).astype(BF16)

    def from_z(d):
        src = lax.rem(z + d, nz)
        return copy(ZX.at[src], ZX.at[src], zx_s.at[d - 1], zx_r.at[src], step(2, d, nz))

    for d in range(1, nz):
        from_z(d).wait_recv()
    whole = ZX[0]
    for i in range(1, nz):
        whole = whole + ZX[i]

    def ifg_part(i, core):
        return ifg_ref.at[:, pl.ds(pl.multiple_of(i * slab + core * lane, lane), lane)]

    ifg_ref[:, pl.ds(pl.multiple_of(y * slab + k * lane, lane), lane)] = whole
    for d in range(1, ny):
        copy(ifg_part(y, k), ifg_part(y, k), yo_s.at[d - 1], yo_r.at[y], step(0, d, ny)).start()

    def core_copy(i, core):
        return copy(ifg_part(i, core), ifg_part(i, core), co_s.at[i], co_r.at[i], partner)

    core_copy(y, k).start()
    for d in range(1, ny):
        by = (d + 1) // 2 if d % 2 else -(d // 2)
        src = lax.rem(y + by + ny, ny)
        copy(ifg_part(src, k), ifg_part(src, k), yo_s.at[0], yo_r.at[src], step(0, 1, ny)).wait_recv()
        core_copy(src, k).start()
    for d in range(1, nx):
        src = lax.rem(x + d, nx)
        copy(gb_part(src), gb_part(src), bo_s.at[d - 1], bo_r.at[src], step(1, d, nx)).wait_recv()
    for i in range(ny):
        core_copy(i, 1 - k).wait_recv()

    def sent(src, ssem, dev):
        copy(src, src, ssem, ssem, dev).wait_send()

    for i in range(last + 1):
        sent(T.at[pl.ds(0, half)], zr_s.at[i], right)
        sent(T.at[pl.ds(0, half)], zl_s.at[i], left)
        sent(T.at[pl.ds(0, half)], dr_s.at[i], partner)
        sent(T.at[pl.ds(0, half)], dl_s.at[i], partner)
    sent(T.at[pl.ds(0, rows)], do_s.at[0], partner)
    for d in range(1, nx):
        dev = step(1, d, nx)
        for i in range(per):
            sent(CT.at[pl.ds(0, unit)], ct_s.at[(d - 1) * per + i], dev)
        sent(NX.at[0], nx_s.at[d - 1], dev)
        sent(AM.at[0], ax_s.at[d - 1], dev)
        sent(SX.at[0], sx_s.at[d - 1], dev)
        sent(BX.at[0], bx_s.at[d - 1], dev)
        sent(gb_part(0), bo_s.at[d - 1], dev)

    def sent_p(chip, _):
        @pl.when(chip // per != x)
        def _():
            p_copy(chip, x, chip // per).wait_send()

        return 0

    lax.fori_loop(0, nz, sent_p, 0)
    for d in range(1, ny):
        dev = step(0, d, ny)
        sent(SY.at[0], sy_s.at[d - 1], dev)
        sent(BY.at[0], by_s.at[d - 1], dev)
        sent(RY.at[0], ry_s.at[d - 1], dev)
        sent(ifg_part(0, 0), yo_s.at[d - 1], dev)
    sent(CX.at[0], cx_s.at[0], partner)
    for d in range(1, nz):
        sent(ZX.at[0], zx_s.at[d - 1], step(2, d, nz))
    for i in range(ny):
        sent(ifg_part(0, 0), co_s.at[i], partner)


def per_device(sizes, tokens, weight, a, b, magnitude, cotangent, lengths):
    ny, nx, nz = sizes
    rows, feats = tokens.shape
    rank, cols = b.shape
    group = rows * 2 * nz
    own = group // nx
    slab = feats // ny
    part = cols // nx
    per = nz // nx
    ring = nz - 1
    V = pltpu.VMEM
    S = lambda n: pltpu.SemaphoreType.DMA((n,))
    pairs = lambda n: [S(n), S(n)]
    outs = pl.pallas_call(
        functools.partial(kernel, sizes),
        out_shape=(
            jax.ShapeDtypeStruct((own, cols), BF16),
            jax.ShapeDtypeStruct((1, cols), F32),
            jax.ShapeDtypeStruct((rank, feats), F32),
            jax.ShapeDtypeStruct((rank, cols), F32),
        ),
        in_specs=[
            pl.BlockSpec(memory_space=pl.ANY),
            pl.BlockSpec(memory_space=pl.ANY),
            pl.BlockSpec(memory_space=pl.ANY),
            pl.BlockSpec(memory_space=pl.ANY),
            pl.BlockSpec(memory_space=pltpu.VMEM),
            pl.BlockSpec(memory_space=pl.ANY),
            pl.BlockSpec(memory_space=pltpu.SMEM),
        ],
        out_specs=[pl.BlockSpec(memory_space=pltpu.VMEM)] * 4,
        scratch_shapes=[
            V((group, feats), BF16),
            V((feats, cols), BF16),
            V((rank, feats), BF16),
            V((rank, cols), BF16),
            V((group, cols), BF16),
            V((group, 128), F32),
            V((group, cols), F32),
            V((group, cols), BF16),
            V((nx, own, cols), BF16),
            V((group, rank), BF16),
            V((nx, 1, cols), F32),
            V((nx, rank, part), F32),
            V((8, cols), F32),
            V((nx, 1, cols), F32),
            V((ny, 1, cols), F32),
            V((1, cols), F32),
            V((1, cols), F32),
            V((rank, cols), F32),
            V((nx, rank, part), F32),
            V((nx, rank, part), F32),
            V((ny, rank, part), F32),
            V((rank, feats), F32),
            V((ny, rank, slab), F32),
            V((ny, rank, slab), F32),
            V((3, rank, slab // 2), F32),
            V((nz, rank, slab // 2), F32),
            V((nx, rank, part), F32),
            S(5),
            *pairs(ring), *pairs(ring), *pairs(ring), *pairs(ring), *pairs(1),
            S((nx - 1) * per), S(nz),
            S(nz), S(nx * per),
            S(nx - 1), S(nx), S(nx - 1), S(nx), S(nx - 1), S(nx),
            S(ny - 1), S(ny),
            S(nx - 1), S(nx),
            S(ny - 1), S(ny),
            S(nx - 1), S(nx),
            S(ny - 1), S(ny),
            *pairs(1),
            S(nz - 1), S(nz),
            S(ny - 1), S(ny),
            *pairs(ny),
        ],
        compiler_params=pltpu.CompilerParams(
            collective_id=0, has_side_effects=True, vmem_limit_bytes=56 * 1024 * 1024
        ),
        name="lora_step",
    )(tokens, weight, a, b, magnitude.reshape(1, cols), cotangent, lengths)
    proj, gmag, ifg, gb = outs
    return proj, gmag.reshape(cols), ifg, gb


def solution(mesh):
    ny, nx = mesh.shape["dp"], mesh.shape["row"]
    nz = mesh.shape["col"] // 2
    split = Mesh(mesh.devices.reshape(ny, nx, nz, 2), AXES)
    return jax.shard_map(
        functools.partial(per_device, (ny, nx, nz)),
        mesh=split,
        in_specs=(
            P(("dp", "z", "core"), "row"),
            P("row", COL),
            P(None, "row"),
            P(None, COL),
            P(COL),
            P(("dp", "row"), COL),
            P("dp", None),
        ),
        out_specs=(P(("dp", "row"), COL), P(COL), P(None, "row"), P(None, COL)),
        check_vma=False,
    )
```

time: 237 us -> 73.4 us (0.31)
  waiting for transfers between devices: 128 us -> 0 us
  Pallas kernels: 0 us -> 66.6 us
  starting transfers between devices: 44.4 us -> 0 us
  blocking collectives: 30.7 us -> 0 us
  local copies, waits for them, and re-layouts: 16.9 us -> 5.85 us
  matrix products: 10.6 us -> 0 us
  other arithmetic: 4.45 us -> 0 us
    all_to_all x7 -> x0, waiting for transfers between devices: 128 us -> none  [the longest x4 91 us: sent_to_all(): return lax.all_to_all(copies, axis, split_axis=0, concat_axis=0, tiled=True)]
    pallas_call x0 -> x1, Pallas kernels: none -> 66.6 us  [per_device(): pl.pallas_call(functools.partial(kernel, sizes), out_shape=(jax.ShapeDtyp...]
    all_to_all x7 -> x0, starting transfers between devices: 44.4 us -> none  [the longest x4 31.4 us: sent_to_all(): return lax.all_to_all(copies, axis, split_axis=0, concat_axis=0, tiled=True)]
    all_to_all x4 -> x0, blocking collectives: 30.7 us -> none  [the longest x3 24.2 us: sent_to_all(): return lax.all_to_all(copies, axis, split_axis=0, concat_axis=0, tiled=True)]
    dot_general x13 -> x0, matrix products: 10.6 us -> none  [the longest x8 4.89 us: contract_product(): lax.dot_general(left, right, (((left_dim,), (right_dim,)), ((), ())), pre...]
    broadcast_in_dim x8 -> x0, local copies, waits for them, and re-layouts: 4.48 us -> none  [the longest x7 4.48 us: sent_to_all(): copies = jnp.broadcast_to(shard, (lax.axis_size(axis), *shard.shape))]
    all_to_all x3 -> x0, local copies, waits for them, and re-layouts: 3.69 us -> none  [the longest x1 2.5 us: sent_to_all(): return lax.all_to_all(copies, axis, split_axis=0, concat_axis=0, tiled=True)]
    unnamed x36 -> x4, local copies, waits for them, and re-layouts: 5.58 us -> 5.85 us
  transfers between devices with their start and end apart: 7 -> 0, of which waited for: 7 -> 0; matrix products, arithmetic and copies ran while one was open for 8% -> 0% of each run, Pallas kernels for 0% -> 0%
where the time goes in v1:
time: 73.4 us; the launch traced here: 73.1 us
  Pallas kernels  66.6 us (91%)
  local copies, waits for them, and re-layouts  5.85 us (8%)
    pallas_call x1, Pallas kernels, per_device(): pl.pallas_call(functools.partial(kernel, sizes), out_shape=(jax.ShapeDtyp...  66.6 us
    unnamed x4, local copies, waits for them, and re-layouts  5.85 us

profile of v1, /device:TPU:1, one launch (start us, length us, event | category | flops | bytes accessed | tf_op | source)
XLA Modules:
  0.0 73.1 jit_solution(14552562176183497950)
XLA Ops:
  0.6 66.6 %lora_step.1 = (bf16[256,512]{1,0:T(8,128)(2,1)}, f32[1,512]{1,0:T(1,128)}, f32[16,2048]{1,0:T(8,128)}, f32[16,512]{1,0:T(8,128)}) custom-call(bf16[64,2048]{1,0:T(8,128)(2,1)} %tok_hbm.1, bf16[2048,512]{1,0:T(8,128)(2,1)} %w_hbm.1, bf16[16,2048]{1,0:T(8,128)(2,1)} %a_hbm.1, bf16[16,512]{1,0:T(8,128)(2,1)} %b_hbm.1, f32[1,512]{1,0:T(1,128)} %bitcast.2, ...), custom_call_target="tpu_custom_call" | custom-call | tf_op jit(solution)/shard_map/lora_step/pallas_call | solution.py:553
  67.2 1.7 %copy.15 = bf16[256,512]{1,0:T(8,128)(2,1)} copy(bf16[256,512]{1,0:T(8,128)(2,1)} %get-tuple-element.16) | data formatting | bytes 524288
  68.9 1.2 %copy.16 = f32[512]{0:T(512)} copy(f32[512]{0:T(512)} %bitcast.3) | data formatting | bytes 4096
  70.1 1.6 %copy.17 = f32[16,2048]{1,0:T(8,128)} copy(f32[16,2048]{1,0:T(8,128)} %get-tuple-element.18) | data formatting | bytes 262144
  71.7 1.4 %copy.18 = f32[16,512]{1,0:T(8,128)} copy(f32[16,512]{1,0:T(8,128)} %get-tuple-element.19) | data formatting | bytes 65536

commit v2 on v1

v2 whole, which is shorter than its diff:
```python
import functools

import jax
import jax.numpy as jnp
from jax import lax
from jax.experimental import pallas as pl
from jax.experimental.pallas import tpu as pltpu
from jax.sharding import Mesh
from jax.sharding import PartitionSpec as P

AXES = ("dp", "row", "z", "core")
COL = ("z", "core")
EPS = 1e-06
F32 = jnp.float32
BF16 = jnp.bfloat16
HIGHEST = lax.Precision.HIGHEST
PIECES = 4
EARLY = 6


def nn(a, b):
    return lax.dot_general(a, b, (((1,), (0,)), ((), ())), preferred_element_type=F32)


def nt(a, b):
    return lax.dot_general(a, b, (((1,), (1,)), ((), ())), preferred_element_type=F32)


def tn(a, b):
    return lax.dot_general(a, b, (((0,), (0,)), ((), ())), preferred_element_type=F32)


def exact(a, b):
    return lax.dot_general(
        a, b, (((1,), (0,)), ((), ())), preferred_element_type=F32, precision=HIGHEST
    )


def far_first(n):
    return sorted(range(1, n), key=lambda d: -min(d, n - d))


def fold(a):
    return jnp.sum(a.reshape(a.shape[0] // 8, 8, a.shape[1]), axis=0)


def kernel(
    sizes,
    tok_hbm, w_hbm, a_hbm, b_hbm, mag_hbm, ct_hbm, lens_hbm,
    proj_ref, gmag_ref, ifg_ref, gb_ref,
    T, W, A, B, CT, WT, PF, PS, PR, DB,
    NX, AX, SACC, SX, SY, SCALE, NORM, BG, BGS, BX, BY, R, RY, H, RL, HL, CX, ZX, AM, MAG, LENS,
    load_sem, zr_s, zr_r, zl_s, zl_r, dr_s, dr_r, dl_s, dl_r, do_s, do_r,
    ct_s, ct_r, p_s, p_r, nx_s, nx_r, ax_s, ax_r, sx_s, sx_r, sy_s, sy_r,
    bx_s, bx_r, by_s, by_r, bo_s, bo_r, ry_s, ry_r, cx_s, cx_r, zx_s, zx_r,
    yo_s, yo_r, co_s, co_r, rl_s, rl_r, wave,
):
    ny, nx, nz = sizes
    y, x, z, k = (lax.axis_index(a) for a in AXES)
    rows = tok_hbm.shape[0]
    piece = rows // PIECES
    unit = 2 * rows
    own = nz // nx * unit
    per = nz // nx
    slab = T.shape[1] // ny
    lane = slab // 2
    part = W.shape[1] // nx

    def at(axis, index):
        return tuple(index if i == axis else v for i, v in enumerate((y, x, z, k)))

    def step(axis, by, n):
        return at(axis, lax.rem((y, x, z)[axis] + by + n, n))

    partner = (y, x, z, 1 - k)
    right = step(2, 1, nz)
    left = step(2, -1, nz)

    def copy(src, dst, ssem, rsem, dev):
        return pltpu.make_async_remote_copy(
            src_ref=src, dst_ref=dst, send_sem=ssem, recv_sem=rsem,
            device_id=dev, device_id_type=pl.DeviceIdType.MESH,
        )

    barrier = pltpu.get_barrier_semaphore()
    near = [partner] + [step(axis, d, n) for axis, n in ((2, nz), (1, nx), (0, ny)) for d in (1, -1)]

    def signal(sem, dev):
        pl.semaphore_signal(sem, inc=1, device_id=dev, device_id_type=pl.DeviceIdType.MESH)

    for dev in near:
        signal(barrier, dev)

    def token_rows(chip, core, h, n):
        return pl.ds(pl.multiple_of(chip * unit + core * rows + h * piece, piece), n)

    mine = token_rows(z, k, 0, rows)
    owned = pl.ds(pl.multiple_of(x * own, own), own)
    loads = [
        pltpu.make_async_copy(tok_hbm, T.at[mine], load_sem.at[0]),
        pltpu.make_async_copy(ct_hbm, CT.at[owned], load_sem.at[1]),
        pltpu.make_async_copy(a_hbm, A, load_sem.at[2]),
        pltpu.make_async_copy(b_hbm, B, load_sem.at[3]),
        pltpu.make_async_copy(w_hbm, W, load_sem.at[4]),
        pltpu.make_async_copy(mag_hbm, MAG, load_sem.at[5]),
        pltpu.make_async_copy(lens_hbm, LENS, load_sem.at[6]),
    ]
    for c in loads:
        c.start()

    seqs = LENS.shape[1]

    def weigh(i, _):
        pos = lax.broadcasted_iota(jnp.int32, (unit, 128), 0) + i * unit
        total = jnp.zeros((unit, 128), F32)
        start = jnp.int32(0)
        for s in range(seqs):
            length = LENS[0, s]
            end = start + length
            inverse = 1.0 / jnp.full((1, 128), length, jnp.int32).astype(F32)
            total += jnp.where((pos >= start) & (pos < end), inverse, 0.0)
            start = end
        WT[pl.ds(pl.multiple_of(i * unit, unit), unit), :] = total
        return 0

    loads[0].wait()
    pl.semaphore_wait(barrier, len(near))

    def ring(right_way, src_chip, h, idx):
        r = token_rows(src_chip, k, h, piece)
        if right_way:
            return copy(T.at[r], T.at[r], zr_s.at[idx], zr_r.at[idx], right)
        return copy(T.at[r], T.at[r], zl_s.at[idx], zl_r.at[idx], left)

    def across(right_way, src_chip, core, h, idx):
        r = token_rows(src_chip, core, h, piece)
        if right_way:
            return copy(T.at[r], T.at[r], dr_s.at[idx], dr_r.at[idx], partner)
        return copy(T.at[r], T.at[r], dl_s.at[idx], dl_r.at[idx], partner)

    def across_own(core):
        r = token_rows(z, core, 0, rows)
        return copy(T.at[r], T.at[r], do_s.at[0], do_r.at[0], partner)

    full = (nz // 2 - 1) * PIECES
    pieces = full + PIECES // 2
    for h in range(PIECES):
        ring(True, z, h, h).start()
        ring(False, z, h, h).start()
    across_own(k).start()

    levels = {0: ny // 2 - 1, 1: nx // 2 - 1, 2: nz // 2 - 1}
    base = {1: 0, 0: levels[1], 2: levels[1] + levels[0]}

    def tell(axis, level):
        for d in (1, -1):
            signal(wave.at[base[axis] + level], step(axis, d, (ny, nx, nz)[axis]))

    def hear(axis, level):
        pl.semaphore_wait(wave.at[base[axis] + level], 2)

    tell(1, 0)
    tell(2, 0)
    loads[6].wait()
    lax.fori_loop(0, nz, weigh, 0)
    for level in range(levels[1]):
        hear(1, level)
        if level + 1 < levels[1]:
            tell(1, level + 1)
    tell(0, 0)

    def spread_word(level):
        for axis in (0, 2):
            if level < levels[axis]:
                hear(axis, level)
            if level + 1 < levels[axis]:
                tell(axis, level + 1)

    def chip_of(j):
        s = (j + 1) // 2
        return lax.rem(z + nz + jnp.where(lax.rem(j, 2) == 1, -s, s), nz)

    def unit_rows(chip):
        return pl.ds(pl.multiple_of(chip * unit, unit), unit)

    def turn_of(chip):
        d = lax.rem(chip - z + nz, nz)
        return jnp.where(d < nz // 2, 2 * d, 2 * (nz - d) - 1)

    ahead = jnp.where(turn_of(x * per) < turn_of(x * per + 1), 0, 1)
    strip = unit // 2
    strips = per * 2 * (nx - 1)

    def ct_copy(loc, part_of, dx, src_x):
        r = pl.ds(pl.multiple_of((src_x * per + loc) * unit + part_of * strip, strip), strip)
        d = lax.rem(dx - src_x + nx, nx)
        return copy(
            CT.at[r], CT.at[r], ct_s.at[(d - 1) * 2 * per + 2 * loc + part_of],
            ct_r.at[src_x * 2 * per + 2 * loc + part_of], at(1, dx),
        )

    def send_ct(n, _):
        u = n // (strips // per)
        loc = jnp.where(u == 0, ahead, 1 - ahead)
        m = lax.rem(n, strips // per)
        ct_copy(loc, m // (nx - 1), lax.rem(x + 1 + lax.rem(m, nx - 1), nx), x).start()
        return 0

    loads[1].wait()
    lax.fori_loop(0, EARLY, send_ct, 0)

    for c in loads[2:6]:
        c.wait()
    chunk = slab

    def norm_part(i, acc):
        c = pl.ds(pl.multiple_of(i * chunk, chunk), chunk)
        m = W[c, :].astype(F32) + tn(A[:, c], B[...])
        return acc + fold(m * m)

    acc = lax.fori_loop(0, ny, norm_part, jnp.zeros((8, W.shape[1]), F32), unroll=4)
    NX[x] = jnp.sum(acc, axis=0, keepdims=True)

    def to_x(src, slot, ssem, rsem, d):
        return copy(src, slot, ssem.at[d - 1], rsem.at[x], step(1, d, nx))

    def from_x(slots, rsem, ssem, d):
        src = lax.rem(x + d, nx)
        return copy(slots.at[src], slots.at[src], ssem.at[d - 1], rsem.at[src], step(1, d, nx))

    for d in range(1, nx):
        to_x(NX.at[x], NX.at[x], nx_s, nx_r, d).start()

    SACC[...] = jnp.zeros_like(SACC)
    BG[...] = jnp.zeros_like(BG)
    R[...] = jnp.zeros_like(R)

    def low_rank():
        am = nn(A[...], W[...]) + exact(nt(A[...], A[...]), B[...].astype(F32))
        for i in range(nx):
            AM[i] = am[:, i * part : (i + 1) * part]
        AX[x] = AM[x]
        for d in range(1, nx):
            dst = lax.rem(x + d, nx)
            copy(AM.at[dst], AX.at[x], ax_s.at[d - 1], ax_r.at[x], step(1, d, nx)).start()

    def project(chip):
        r = unit_rows(chip)
        t = T[r, :]
        down = nt(t, A[...]).astype(BF16)
        p = nn(t, W[...]) + nn(down, B[...])
        DB[r, :] = down
        PF[r, :] = p
        PS[r, :] = p.astype(BF16)

    def need_ct(chip):
        @pl.when(chip // per != x)
        def _():
            for h in range(2):
                ct_copy(lax.rem(chip, per), h, x, chip // per).wait_recv()

    def weighted(chip):
        r = unit_rows(chip)
        w = WT[r, :]
        return CT[r, :].astype(F32) * jnp.concatenate([w] * (W.shape[1] // 128), axis=1)

    def scale_sum(chip):
        SACC[...] += fold(weighted(chip) * PF[unit_rows(chip), :])

    def backward(chip):
        r = unit_rows(chip)
        gp = (weighted(chip) * SCALE[...]).astype(BF16)
        BG[...] += tn(DB[r, :], gp)
        back = nt(B[...], gp)
        high = back.astype(BF16)
        low = (back - high.astype(F32)).astype(BF16)
        both = nn(jnp.concatenate([high, low], axis=0), T[r, :])
        R[...] += both[: back.shape[0]] + both[back.shape[0] :]

    def p_copy(chip, src, dst):
        loc = lax.rem(chip, per)
        r = pl.ds(pl.multiple_of(loc * unit, unit), unit)
        return copy(
            PS.at[unit_rows(chip)], PR.at[src, r], p_s.at[chip], p_r.at[src * per + loc], at(1, dst)
        )

    def send_p(chip):
        @pl.when(chip // per != x)
        def _():
            p_copy(chip, x, chip // per).start()

    def handle(i):
        s = i // PIECES + 1
        h = lax.rem(i, PIECES)
        far = i >= full
        other = PIECES // 2
        hl = jnp.where(far, h + other, h)
        fr = lax.rem(z - s + nz, nz)
        fl = lax.rem(z + s, nz)
        third = i >= full - PIECES
        ring(True, fr, h, i).wait_recv()

        @pl.when((i < full - PIECES) | (third & (h < other) & (i < full)))
        def _():
            ring(True, fr, h, i + PIECES).start()

        across(True, fr, k, h, i).start()
        ring(False, fl, hl, i).wait_recv()

        @pl.when((i < full - PIECES) | (third & (h >= other) & (i < full)))
        def _():
            ring(False, fl, hl, jnp.where(third, i + PIECES - other, i + PIECES)).start()

        across(False, fl, k, hl, i).start()

        @pl.when(i + EARLY < strips)
        def _():
            send_ct(i + EARLY, 0)

    def need_tokens(j):
        chip = chip_of(j)

        @pl.when(j == 0)
        def _():
            across_own(1 - k).wait_recv()

        @pl.when((lax.rem(j, 2) == 1) & (j < nz - 1))
        def _():
            for h in range(PIECES):
                across(True, chip, 1 - k, h, (j - 1) // 2 * PIECES + h).wait_recv()

        @pl.when((lax.rem(j, 2) == 0) & (j > 0))
        def _():
            for h in range(PIECES):
                across(False, chip, 1 - k, h, (j - 2) // 2 * PIECES + h).wait_recv()

        @pl.when(j == nz - 1)
        def _():
            for h in range(PIECES // 2):
                across(True, chip, 1 - k, h, full + h).wait_recv()
                across(False, chip, 1 - k, h + PIECES // 2, full + h).wait_recv()

    def handle_range(low, high):
        def one(i, _):
            handle(i)
            return 0

        lax.fori_loop(low, high, one, 0)

    held = nz - 3

    def settle(j, _):
        c = chip_of(j)
        need_ct(c)
        scale_sum(c)
        backward(c)
        return 0

    def turn(j, _):
        chip = chip_of(j)
        need_tokens(j)
        project(chip)

        @pl.when(j == 1)
        def _():
            for d in range(1, nx):
                from_x(NX, nx_r, nx_s, d).wait_recv()
            sq = NX[0]
            for i in range(1, nx):
                sq = sq + NX[i]
            norm = jnp.sqrt(sq + EPS)
            NORM[...] = norm
            SCALE[...] = MAG[...] / norm

        mid = j < nz - 3
        inner = jnp.where(mid, PIECES // 2 * (j + 1), jnp.where(j == nz - 3, full, pieces - 1))
        outer = jnp.where(mid, inner + PIECES // 2, jnp.where(j == nz - 3, pieces - 1, pieces))
        handle_range(jnp.where(j == 0, 0, inner), jnp.where(j == 0, PIECES, jnp.where(j == nz - 1, inner, outer)))

        @pl.when(j == 0)
        def _():
            low_rank()

        for level in range(max(levels.values())):

            @pl.when(j == level)
            def _():
                spread_word(level)

        @pl.when(j < held)
        def _():
            send_p(chip)

        low = jnp.where(j == nz - 2, nz - 5, j - 2)
        high = jnp.where(j == nz - 2, nz - 2, jnp.where((j >= 2) & (j < nz - 3), j - 1, low))
        lax.fori_loop(low, high, settle, 0)

        @pl.when(j == nz - 2)
        def _():
            for i in range(ny):
                H[i] = R[:, i * slab : (i + 1) * slab]
            R[...] = jnp.zeros_like(R)
            RY[y] = H[y]
            for d in far_first(ny):
                dst = lax.rem(y + d, ny)
                copy(H.at[dst], RY.at[y], ry_s.at[d - 1], ry_r.at[y], step(0, d, ny)).start()

        return 0

    lax.fori_loop(0, nz, turn, 0)

    def finish_s(j, _):
        c = chip_of(j)
        need_ct(c)
        scale_sum(c)
        return 0

    lax.fori_loop(nz - 2, nz, finish_s, 0)
    SX[x] = jnp.sum(SACC[...], axis=0, keepdims=True)
    for d in far_first(nx):
        to_x(SX.at[x], SX.at[x], sx_s, sx_r, d).start()

    def finish_b(j, _):
        backward(chip_of(j))
        return 0

    lax.fori_loop(nz - 2, nz, finish_b, 0)
    for i in range(ny):
        HL[i] = R[:, i * slab : (i + 1) * slab].astype(BF16)
    RL[y] = HL[y]
    for d in far_first(ny):
        dst = lax.rem(y + d, ny)
        copy(HL.at[dst], RL.at[y], rl_s.at[d - 1], rl_r.at[y], step(0, d, ny)).start()
    for i in range(nx):
        BGS[i] = BG[:, i * part : (i + 1) * part]
    BX[x] = BGS[x]

    for d in range(1, nx):
        from_x(SX, sx_r, sx_s, d).wait_recv()
    sx = SX[0]
    for i in range(1, nx):
        sx = sx + SX[i]
    SY[y] = sx

    def to_y(src, slot, ssem, rsem, d):
        return copy(src, slot, ssem.at[d - 1], rsem.at[y], step(0, d, ny))

    def from_y(slots, rsem, ssem, d):
        src = lax.rem(y + d, ny)
        return copy(slots.at[src], slots.at[src], ssem.at[d - 1], rsem.at[src], step(0, d, ny))

    for d in far_first(ny):
        to_y(SY.at[y], SY.at[y], sy_s, sy_r, d).start()
    for d in range(1, nx):
        dst = lax.rem(x + d, nx)
        copy(BGS.at[dst], BX.at[x], bx_s.at[d - 1], bx_r.at[x], step(1, d, nx)).start()

    def send_held(j, _):
        send_p(chip_of(j))
        return 0

    lax.fori_loop(held, nz, send_held, 0)

    for d in range(1, ny):
        from_y(RY, ry_r, ry_s, d).wait_recv()
    row_part = RY[0]
    for i in range(1, ny):
        row_part = row_part + RY[i]
    norm = NORM[...]
    inverse = 1.0 / norm
    slope = -MAG[...] * (inverse * inverse * inverse)

    for d in range(1, ny):
        from_y(SY, sy_r, sy_s, d).wait_recv()
    s_all = SY[0]
    for i in range(1, ny):
        s_all = s_all + SY[i]
    coef = s_all * slope
    scaled = (B[...].astype(F32) * coef).astype(BF16)
    cols = pl.ds(pl.multiple_of(y * slab, slab), slab)
    part_y = nt(scaled, W[cols, :]) + exact(nt(scaled, B[...]), A[:, cols].astype(F32))
    for d in range(1, ny):
        from_y(RL, rl_r, rl_s, d).wait_recv()
    for i in range(ny):
        row_part = row_part + RL[i].astype(F32)
    part_y = part_y + row_part

    CX[0] = part_y[:, :lane]
    CX[1] = part_y[:, lane:]
    cross = copy(CX.at[1 - k], CX.at[2], cx_s.at[0], cx_r.at[0], partner)
    cross.start()
    cross.wait_recv()
    ZX[z] = CX[k] + CX[2]

    def to_z(d):
        return copy(ZX.at[z], ZX.at[z], zx_s.at[d - 1], zx_r.at[z], step(2, d, nz))

    for d in far_first(nz):
        to_z(d).start()
    gmag_ref[...] = s_all * inverse

    for d in range(1, nx):
        from_x(BX, bx_r, bx_s, d).wait_recv()
    bx = BX[0]
    for i in range(1, nx):
        bx = bx + BX[i]
    BY[y] = bx
    for d in far_first(ny):
        to_y(BY.at[y], BY.at[y], by_s, by_r, d).start()
    for d in range(1, nx):
        from_x(AX, ax_r, ax_s, d).wait_recv()
    a_all = AX[0]
    for i in range(1, nx):
        a_all = a_all + AX[i]

    for d in range(1, nx):
        src = lax.rem(x + d, nx)
        for loc in range(per):
            p_copy(x * per + loc, src, src).wait_recv()
    rest = pl.ds(pl.multiple_of(x * own, own), own)
    total = PF[rest, :]
    for d in range(1, nx):
        total = total + PR[lax.rem(x + d, nx)].astype(F32)
    proj_ref[...] = (total * SCALE[...]).astype(BF16)

    def from_z(d):
        src = lax.rem(z + d, nz)
        return copy(ZX.at[src], ZX.at[src], zx_s.at[d - 1], zx_r.at[src], step(2, d, nz))

    for d in range(1, nz):
        from_z(d).wait_recv()
    whole = ZX[0]
    for i in range(1, nz):
        whole = whole + ZX[i]

    def ifg_part(i, core):
        return ifg_ref.at[:, pl.ds(pl.multiple_of(i * slab + core * lane, lane), lane)]

    ifg_ref[:, pl.ds(pl.multiple_of(y * slab + k * lane, lane), lane)] = whole
    for d in far_first(ny):
        copy(ifg_part(y, k), ifg_part(y, k), yo_s.at[d - 1], yo_r.at[y], step(0, d, ny)).start()

    def core_copy(i, core):
        return copy(ifg_part(i, core), ifg_part(i, core), co_s.at[i], co_r.at[i], partner)

    core_copy(y, k).start()

    for d in range(1, ny):
        from_y(BY, by_r, by_s, d).wait_recv()
    b_all = BY[0]
    for i in range(1, ny):
        b_all = b_all + BY[i]

    for i in range(nx):

        @pl.when(x == i)
        def _():
            c = slice(i * part, (i + 1) * part)
            gb_ref[:, c] = b_all + a_all * coef[:, c]

    def gb_part(i):
        return gb_ref.at[:, pl.ds(pl.multiple_of(i * part, part), part)]

    for d in range(1, nx):
        copy(gb_part(x), gb_part(x), bo_s.at[d - 1], bo_r.at[x], step(1, d, nx)).start()

    for d in range(1, ny):
        by = (d + 1) // 2 if d % 2 else -(d // 2)
        src = lax.rem(y + by + ny, ny)
        copy(ifg_part(src, k), ifg_part(src, k), yo_s.at[0], yo_r.at[src], step(0, 1, ny)).wait_recv()
        core_copy(src, k).start()
    for d in range(1, nx):
        src = lax.rem(x + d, nx)
        copy(gb_part(src), gb_part(src), bo_s.at[d - 1], bo_r.at[src], step(1, d, nx)).wait_recv()
    for i in range(ny):
        core_copy(i, 1 - k).wait_recv()

    def sent(src, ssem, dev):
        copy(src, src, ssem, ssem, dev).wait_send()

    for i in range(pieces):
        sent(T.at[pl.ds(0, piece)], zr_s.at[i], right)
        sent(T.at[pl.ds(0, piece)], zl_s.at[i], left)
        sent(T.at[pl.ds(0, piece)], dr_s.at[i], partner)
        sent(T.at[pl.ds(0, piece)], dl_s.at[i], partner)
    sent(T.at[pl.ds(0, rows)], do_s.at[0], partner)
    for d in range(1, nx):
        dev = step(1, d, nx)
        for i in range(2 * per):
            sent(CT.at[pl.ds(0, strip)], ct_s.at[(d - 1) * 2 * per + i], dev)
        sent(NX.at[0], nx_s.at[d - 1], dev)
        sent(AM.at[0], ax_s.at[d - 1], dev)
        sent(SX.at[0], sx_s.at[d - 1], dev)
        sent(BX.at[0], bx_s.at[d - 1], dev)
        sent(gb_part(0), bo_s.at[d - 1], dev)

    def sent_p(chip, _):
        @pl.when(chip // per != x)
        def _():
            p_copy(chip, x, chip // per).wait_send()

        return 0

    lax.fori_loop(0, nz, sent_p, 0)
    for d in range(1, ny):
        dev = step(0, d, ny)
        sent(SY.at[0], sy_s.at[d - 1], dev)
        sent(BY.at[0], by_s.at[d - 1], dev)
        sent(RY.at[0], ry_s.at[d - 1], dev)
        sent(RL.at[0], rl_s.at[d - 1], dev)
        sent(ifg_part(0, 0), yo_s.at[d - 1], dev)
    sent(CX.at[0], cx_s.at[0], partner)
    for d in range(1, nz):
        sent(ZX.at[0], zx_s.at[d - 1], step(2, d, nz))
    for i in range(ny):
        sent(ifg_part(0, 0), co_s.at[i], partner)


def put_out(*refs):
    *pairs, sem = refs
    copies = [pltpu.make_async_copy(pairs[i], pairs[i + 4], sem.at[i]) for i in range(4)]
    for c in copies:
        c.start()
    for c in copies:
        c.wait()


def per_device(sizes, tokens, weight, a, b, magnitude, cotangent, lengths):
    ny, nx, nz = sizes
    rows, feats = tokens.shape
    rank, cols = b.shape
    group = rows * 2 * nz
    own = group // nx
    slab = feats // ny
    part = cols // nx
    per = nz // nx
    ring = (nz // 2 - 1) * PIECES + PIECES // 2
    words = ny // 2 + nx // 2 + nz // 2 - 3
    V = pltpu.VMEM
    S = lambda n: pltpu.SemaphoreType.DMA((n,))
    pairs = lambda n: [S(n), S(n)]
    outs = pl.pallas_call(
        functools.partial(kernel, sizes),
        out_shape=(
            V((own, cols), BF16),
            V((1, cols), F32),
            V((rank, feats), F32),
            V((rank, cols), F32),
        ),
        in_specs=[pl.BlockSpec(memory_space=pl.ANY)] * 7,
        out_specs=[pl.BlockSpec(memory_space=pltpu.VMEM)] * 4,
        scratch_shapes=[
            V((group, feats), BF16),
            V((feats, cols), BF16),
            V((rank, feats), BF16),
            V((rank, cols), BF16),
            V((group, cols), BF16),
            V((group, 128), F32),
            V((group, cols), F32),
            V((group, cols), BF16),
            V((nx, own, cols), BF16),
            V((group, rank), BF16),
            V((nx, 1, cols), F32),
            V((nx, rank, part), F32),
            V((8, cols), F32),
            V((nx, 1, cols), F32),
            V((ny, 1, cols), F32),
            V((1, cols), F32),
            V((1, cols), F32),
            V((rank, cols), F32),
            V((nx, rank, part), F32),
            V((nx, rank, part), F32),
            V((ny, rank, part), F32),
            V((rank, feats), F32),
            V((ny, rank, slab), F32),
            V((ny, rank, slab), F32),
            V((ny, rank, slab), BF16),
            V((ny, rank, slab), BF16),
            V((3, rank, slab // 2), F32),
            V((nz, rank, slab // 2), F32),
            V((nx, rank, part), F32),
            V((1, cols), F32),
            pltpu.SMEM(lengths.shape, jnp.int32),
            S(7),
            *pairs(ring), *pairs(ring), *pairs(ring), *pairs(ring), *pairs(1),
            S((nx - 1) * 2 * per), S(2 * nz),
            S(nz), S(nx * per),
            S(nx - 1), S(nx), S(nx - 1), S(nx), S(nx - 1), S(nx),
            S(ny - 1), S(ny),
            S(nx - 1), S(nx),
            S(ny - 1), S(ny),
            S(nx - 1), S(nx),
            S(ny - 1), S(ny),
            *pairs(1),
            S(nz - 1), S(nz),
            S(ny - 1), S(ny),
            *pairs(ny),
            S(ny - 1), S(ny),
            pltpu.SemaphoreType.REGULAR((words,)),
        ],
        compiler_params=pltpu.CompilerParams(
            collective_id=0, has_side_effects=True, vmem_limit_bytes=56 * 1024 * 1024
        ),
        name="lora_step",
    )(tokens, weight, a, b, magnitude.reshape(1, cols), cotangent, lengths)
    whole = [jax.ShapeDtypeStruct(o.shape, o.dtype) for o in outs]
    proj, gmag, ifg, gb = pl.pallas_call(
        put_out,
        out_shape=whole,
        in_specs=[pl.BlockSpec(memory_space=pltpu.VMEM)] * 4,
        out_specs=[pl.BlockSpec(memory_space=pl.ANY)] * 4,
        scratch_shapes=[S(4)],
        compiler_params=pltpu.CompilerParams(vmem_limit_bytes=1024 * 1024),
        name="put_out",
    )(*outs)
    return proj, gmag.reshape(cols), ifg, gb


def solution(mesh):
    ny, nx = mesh.shape["dp"], mesh.shape["row"]
    nz = mesh.shape["col"] // 2
    split = Mesh(mesh.devices.reshape(ny, nx, nz, 2), AXES)
    return jax.shard_map(
        functools.partial(per_device, (ny, nx, nz)),
        mesh=split,
        in_specs=(
            P(("dp", "z", "core"), "row"),
            P("row", COL),
            P(None, "row"),
            P(None, COL),
            P(COL),
            P(("dp", "row"), COL),
            P("dp", None),
        ),
        out_specs=(P(("dp", "row"), COL), P(COL), P(None, "row"), P(None, COL)),
        check_vma=False,
    )
```

time: 73.4 us -> 65.4 us (0.89)
  the two profiles are of different devices: /device:TPU:1 before, /device:TPU:5 now
where the time goes in v2:
time: 65.4 us; the launch traced here: 65.2 us
  Pallas kernels  64.6 us (99%)
    pallas_call x1, Pallas kernels, per_device(): pl.pallas_call(functools.partial(kernel, sizes), out_shape=(V((own, cols)...  63.8 us

profile of v2, /device:TPU:5, one launch (start us, length us, event | category | flops | bytes accessed | tf_op | source)
XLA Modules:
  0.0 65.2 jit_solution(16163261225779670244)
XLA Ops:
  0.6 63.8 %lora_step.1 = (bf16[256,512]{1,0:T(8,128)(2,1)S(1)}, f32[1,512]{1,0:T(1,128)S(1)}, f32[16,2048]{1,0:T(8,128)S(1)}, f32[16,512]{1,0:T(8,128)S(1)}) custom-call(bf16[64,2048]{1,0:T(8,128)(2,1)} %tok_hbm.1, bf16[2048,512]{1,0:T(8,128)(2,1)} %w_hbm.1, bf16[16,2048]{1,0:T(8,128)(2,1)} %a_hbm.1, bf16[16,512]{1,0:T(8,128)(2,1)} %b_hbm.1, f32[1,512]{1,0:T(1,128)} %bitcast.2, ...), custom_call_target="tpu_custom_call" | custom-call | tf_op jit(solution)/shard_map/lora_step/pallas_call | solution.py:642
  64.4 0.8 %put_out.1 = (bf16[256,512]{1,0:T(8,128)(2,1)}, f32[1,512]{1,0:T(1,128)}, f32[16,2048]{1,0:T(8,128)}, f32[16,512]{1,0:T(8,128)}) custom-call(bf16[256,512]{1,0:T(8,128)(2,1)S(1)} %get-tuple-element.12.refs_0_, f32[1,512]{1,0:T(1,128)S(1)} %get-tuple-element.13.refs_1_, f32[16,2048]{1,0:T(8,128)S(1)} %get-tuple-element.14.refs_2_, ...), custom_call_target="tpu_custom_call" | custom-call | tf_op jit(solution)/shard_map/put_out/pallas_call | solution.py:707

commit v3 on v2

v3 whole, which is shorter than its diff:
```python
import functools

import jax
import jax.numpy as jnp
from jax import lax
from jax.experimental import pallas as pl
from jax.experimental.pallas import tpu as pltpu
from jax.sharding import Mesh
from jax.sharding import PartitionSpec as P

AXES = ("dp", "row", "z", "core")
COL = ("z", "core")
EPS = 1e-06
F32 = jnp.float32
BF16 = jnp.bfloat16
HIGHEST = lax.Precision.HIGHEST
HELD = 5
PIECES = 4
EARLY = 6


LEAVE = ("zr", "zl", "d", "own", "ct", "p", "nx", "ax", "s", "bx", "by", "bo", "ry", "rl", "zx", "if")
ENTER = ("p", "nx", "ax", "s", "bx", "by", "bo", "ry", "rl", "zx", "if")


def nn(a, b):
    return lax.dot_general(a, b, (((1,), (0,)), ((), ())), preferred_element_type=F32)


def nt(a, b):
    return lax.dot_general(a, b, (((1,), (1,)), ((), ())), preferred_element_type=F32)


def tn(a, b):
    return lax.dot_general(a, b, (((0,), (0,)), ((), ())), preferred_element_type=F32)


def exact(a, b):
    return lax.dot_general(
        a, b, (((1,), (0,)), ((), ())), preferred_element_type=F32, precision=HIGHEST
    )


def far_first(n):
    return sorted(range(1, n), key=lambda d: -min(d, n - d))


def fold(a):
    return jnp.sum(a.reshape(a.shape[0] // 8, 8, a.shape[1]), axis=0)


def kernel(
    sizes,
    tok_hbm, w_hbm, a_hbm, b_hbm, mag_hbm, ct_hbm, lens_hbm,
    proj_ref, gmag_ref, ifg_ref, gb_ref,
    T, W, A, B, CT, WT, PF, PS, PR, PV, DB,
    NX, AX, SACC, SS, SCALE, NORM, BG, BGS, BX, BY, R, RY, H, RL, HL, CX, ZX, IF, AM, WX, MAG, LENS,
    load_sem, zr_r, zl_r, d_r, ct_r, pv_r, out_sem, in_sem, wave,
):
    ny, nx, nz = sizes
    y, x, z, k = (lax.axis_index(a) for a in AXES)
    rows = tok_hbm.shape[0]
    piece = rows // PIECES
    unit = 2 * rows
    own = nz // nx * unit
    per = nz // nx
    slab = T.shape[1] // ny
    lane = slab // 2
    part = W.shape[1] // nx

    def at(axis, index):
        return tuple(index if i == axis else v for i, v in enumerate((y, x, z, k)))

    def step(axis, by, n):
        return at(axis, lax.rem((y, x, z)[axis] + by + n, n))

    def leave(name):
        return out_sem.at[LEAVE.index(name)]

    def enter(name):
        return in_sem.at[ENTER.index(name)]

    partner = (y, x, z, 1 - k)
    right = step(2, 1, nz)
    left = step(2, -1, nz)

    def copy(src, dst, ssem, rsem, dev):
        return pltpu.make_async_remote_copy(
            src_ref=src, dst_ref=dst, send_sem=ssem, recv_sem=rsem,
            device_id=dev, device_id_type=pl.DeviceIdType.MESH,
        )

    def arrived(sem, ref):
        copy(ref, ref, sem, sem, partner).wait_recv()

    barrier = pltpu.get_barrier_semaphore()
    near = [partner] + [step(axis, d, n) for axis, n in ((2, nz), (1, nx), (0, ny)) for d in (1, -1)]

    def signal(sem, dev):
        pl.semaphore_signal(sem, inc=1, device_id=dev, device_id_type=pl.DeviceIdType.MESH)

    for dev in near:
        signal(barrier, dev)

    def token_rows(chip, core, h, n):
        return pl.ds(pl.multiple_of(chip * unit + core * rows + h * piece, piece), n)

    mine = token_rows(z, k, 0, rows)
    owned = pl.ds(pl.multiple_of(x * own, own), own)
    loads = [
        pltpu.make_async_copy(tok_hbm, T.at[mine], load_sem.at[0]),
        pltpu.make_async_copy(ct_hbm, CT.at[owned], load_sem.at[1]),
        pltpu.make_async_copy(a_hbm, A, load_sem.at[2]),
        pltpu.make_async_copy(b_hbm, B, load_sem.at[3]),
        pltpu.make_async_copy(w_hbm, W, load_sem.at[4]),
        pltpu.make_async_copy(mag_hbm, MAG, load_sem.at[5]),
        pltpu.make_async_copy(lens_hbm, LENS, load_sem.at[6]),
    ]
    for c in loads:
        c.start()

    seqs = LENS.shape[1]

    def weigh(i, _):
        pos = lax.broadcasted_iota(jnp.int32, (unit, 128), 0) + i * unit
        total = jnp.zeros((unit, 128), F32)
        start = jnp.int32(0)
        for s in range(seqs):
            length = LENS[0, s]
            end = start + length
            inverse = 1.0 / jnp.full((1, 128), length, jnp.int32).astype(F32)
            total += jnp.where((pos >= start) & (pos < end), inverse, 0.0)
            start = end
        WT[pl.ds(pl.multiple_of(i * unit, unit), unit), :] = total
        return 0

    loads[0].wait()
    pl.semaphore_wait(barrier, len(near))

    def ring(right_way, src_chip, h, idx):
        r = token_rows(src_chip, k, h, piece)
        if right_way:
            return copy(T.at[r], T.at[r], leave("zr"), zr_r.at[idx], right)
        return copy(T.at[r], T.at[r], leave("zl"), zl_r.at[idx], left)

    def across(src_chip, h, j):
        r = token_rows(src_chip, k, h, piece)
        return copy(T.at[r], T.at[r], leave("d"), d_r.at[j], partner)

    full = (nz // 2 - 1) * PIECES
    pieces = full + PIECES // 2
    for h in range(PIECES):
        ring(True, z, h, h).start()
        ring(False, z, h, h).start()
    copy(T.at[mine], T.at[mine], leave("own"), d_r.at[0], partner).start()

    levels = {0: ny // 2, 1: nx // 2 - 1, 2: nz // 2 - 1}
    base = {1: 0, 0: levels[1], 2: levels[1] + levels[0]}

    def tell(axis, level):
        for d in (1, -1):
            signal(wave.at[base[axis] + level], step(axis, d, (ny, nx, nz)[axis]))

    def hear(axis, level):
        pl.semaphore_wait(wave.at[base[axis] + level], 2)

    tell(1, 0)
    tell(2, 0)
    loads[6].wait()
    lax.fori_loop(0, nz, weigh, 0)
    def spread_word(level):
        for axis in (0, 2):
            if level < levels[axis]:
                hear(axis, level)
            if level + 1 < levels[axis]:
                tell(axis, level + 1)

    def chip_of(j):
        s = (j + 1) // 2
        return lax.rem(z + nz + jnp.where(lax.rem(j, 2) == 1, -s, s), nz)

    def unit_rows(chip):
        return pl.ds(pl.multiple_of(chip * unit, unit), unit)

    def turn_of(chip):
        d = lax.rem(chip - z + nz, nz)
        return jnp.where(d < nz // 2, 2 * d, 2 * (nz - d) - 1)

    ahead = jnp.where(turn_of(x * per) < turn_of(x * per + 1), 0, 1)
    strip = unit // 2
    strips = per * 2 * (nx - 1)

    def ct_copy(loc, part_of, dx, src_x):
        r = pl.ds(pl.multiple_of((src_x * per + loc) * unit + part_of * strip, strip), strip)
        d = lax.rem(dx - src_x + nx, nx)
        return copy(CT.at[r], CT.at[r], leave("ct"), ct_r.at[src_x * per + loc], at(1, dx))

    def send_ct(n, _):
        u = n // (strips // per)
        loc = jnp.where(u == 0, ahead, 1 - ahead)
        m = lax.rem(n, strips // per)
        ct_copy(loc, m // (nx - 1), lax.rem(x + 1 + lax.rem(m, nx - 1), nx), x).start()
        return 0

    for c in loads[2:6]:
        c.wait()
    chunk = slab

    def norm_part(i, acc):
        c = pl.ds(pl.multiple_of(i * chunk, chunk), chunk)
        m = W[c, :].astype(F32) + tn(A[:, c], B[...])
        return acc + fold(m * m)

    acc = lax.fori_loop(0, ny, norm_part, jnp.zeros((8, W.shape[1]), F32), unroll=4)
    NX[x] = jnp.sum(acc, axis=0, keepdims=True)
    for level in range(levels[1]):
        hear(1, level)
        if level + 1 < levels[1]:
            tell(1, level + 1)
    tell(0, 0)
    loads[1].wait()

    def to_x(name, src, slot, d):
        return copy(src, slot, leave(name), enter(name), step(1, d, nx))

    def to_y(name, src, slot, d):
        return copy(src, slot, leave(name), enter(name), step(0, d, ny))

    for d in range(1, nx):
        to_x("nx", NX.at[x], NX.at[x], d).start()
    lax.fori_loop(0, EARLY, send_ct, 0)

    SACC[...] = jnp.zeros_like(SACC)
    BG[...] = jnp.zeros_like(BG)
    R[...] = jnp.zeros_like(R)

    def low_rank():
        am = nn(A[...], W[...]) + exact(nt(A[...], A[...]), B[...].astype(F32))
        for i in range(nx):
            AM[i] = am[:, i * part : (i + 1) * part]
        AX[x] = AM[x]
        for d in range(1, nx):
            dst = lax.rem(x + d, nx)
            to_x("ax", AM.at[dst], AX.at[x], d).start()

    def project(chip):
        r = unit_rows(chip)
        t = T[r, :]
        down = nt(t, A[...]).astype(BF16)
        p = nn(t, W[...]) + nn(down, B[...])
        DB[r, :] = down
        PF[r, :] = p
        PS[r, :] = p.astype(BF16)

    def need_ct(chip):
        @pl.when(chip // per != x)
        def _():
            arrived(ct_r.at[chip], CT.at[unit_rows(chip)])

    def weighted(chip):
        r = unit_rows(chip)
        w = WT[r, :]
        return CT[r, :].astype(F32) * jnp.concatenate([w] * (W.shape[1] // 128), axis=1)

    def scale_sum(chip):
        SACC[...] += fold(weighted(chip) * PF[unit_rows(chip), :])

    def backward(chip):
        r = unit_rows(chip)
        gp = (weighted(chip) * SCALE[...]).astype(BF16)
        BG[...] += tn(DB[r, :], gp)
        back = nt(B[...], gp)
        high = back.astype(BF16)
        low = (back - high.astype(F32)).astype(BF16)
        both = nn(jnp.concatenate([high, low], axis=0), T[r, :])
        R[...] += both[: back.shape[0]] + both[back.shape[0] :]

    def to_owner(chip):
        return lax.rem(chip // per - x + nx, nx)

    passes_on = jnp.where(k == 0, 1, nx - 1)

    def slot_of(chip):
        return pl.ds(pl.multiple_of(lax.rem(chip, per) * unit, unit), unit)

    def p_out(chip):
        side = jnp.where(to_owner(chip) == 1, 0, 1)
        dst = PR.at[side, slot_of(chip)]
        return copy(PS.at[unit_rows(chip)], dst, leave("p"), enter("p"), at(1, chip // per))

    def send_p(chip):
        @pl.when((to_owner(chip) == nx - passes_on))
        def _():
            p_out(chip).start()

        @pl.when(to_owner(chip) == 2)
        def _():
            dev = at(1, lax.rem(x + passes_on, nx))
            dst = PV.at[slot_of(chip)]
            copy(PS.at[unit_rows(chip)], dst, leave("p"), pv_r.at[lax.rem(chip, per)], dev).start()

    def pass_on(chip):
        @pl.when(to_owner(chip) == passes_on)
        def _():
            slot = slot_of(chip)
            arrived(pv_r.at[lax.rem(chip, per)], PV.at[slot])
            r = unit_rows(chip)
            PS[r, :] = (PF[r, :] + PV[slot, :].astype(F32)).astype(BF16)
            p_out(chip).start()

    def handle(i):
        s = i // PIECES + 1
        h = lax.rem(i, PIECES)
        far = i >= full
        other = PIECES // 2
        hl = jnp.where(far, h + other, h)
        fr = lax.rem(z - s + nz, nz)
        fl = lax.rem(z + s, nz)
        third = i >= full - PIECES
        ring(True, fr, h, i).wait_recv()
        across(fr, h, jnp.where(far, nz - 1, 2 * s - 1)).start()

        @pl.when((i < full - PIECES) | (third & (h < other) & (i < full)))
        def _():
            ring(True, fr, h, i + PIECES).start()

        ring(False, fl, hl, i).wait_recv()
        across(fl, hl, jnp.where(far, nz - 1, 2 * s)).start()

        @pl.when((i < full - PIECES) | (third & (h >= other) & (i < full)))
        def _():
            ring(False, fl, hl, jnp.where(third, i + PIECES - other, i + PIECES)).start()

        @pl.when(i + EARLY < strips)
        def _():
            send_ct(i + EARLY, 0)

    def need_tokens(j):
        arrived(d_r.at[j], T.at[token_rows(chip_of(j), 1 - k, 0, rows)])

    def handle_range(low, high):
        def one(i, _):
            handle(i)
            return 0

        lax.fori_loop(low, high, one, 0)

    held = HELD

    def settle(j, _):
        c = chip_of(j)
        need_ct(c)
        scale_sum(c)
        backward(c)
        return 0

    def slice_weights():
        cols = pl.ds(pl.multiple_of(y * slab, slab), slab)
        wide = W.shape[1]
        low_rank_t = tn(B[...], A[:, cols])
        high = low_rank_t.astype(BF16)
        WX[:wide, :] = W[cols, :].astype(F32).T.astype(BF16)
        WX[wide : 2 * wide, :] = high
        WX[2 * wide :, :] = (low_rank_t - high.astype(F32)).astype(BF16)

    need_tokens(0)
    project(z)
    handle_range(0, PIECES // 4)
    low_rank()
    handle_range(PIECES // 4, 3 * PIECES // 4)
    slice_weights()
    handle_range(3 * PIECES // 4, PIECES)
    send_p(z)

    def turn(j, _):
        s = (j + 1) // 2
        odd = lax.rem(j, 2)
        chip = chip_of(j)

        @pl.when(odd == 1)
        def _():
            handle(s * PIECES)

        need_tokens(j)
        project(chip)

        @pl.when(j == 1)
        def _():
            arrived(enter("nx"), NX.at[pl.ds(0, nx - 1)])
            sq = NX[0]
            for i in range(1, nx):
                sq = sq + NX[i]
            norm = jnp.sqrt(sq + EPS)
            NORM[...] = norm
            SCALE[...] = MAG[...] / norm

        mid = s * PIECES + PIECES // 2
        low = jnp.minimum(jnp.where(odd == 1, s * PIECES + 1, mid), pieces)
        high = jnp.minimum(jnp.where(odd == 1, mid, mid + 1), pieces)
        handle_range(low, high)

        for level in range(max(levels.values())):

            @pl.when(j == level + 1)
            def _():
                spread_word(level)

        @pl.when(j < held)
        def _():
            send_p(chip)

        @pl.when((j >= 2) & (j < nz - 3))
        def _():
            settle(j - 2, 0)

        handle_range(high, jnp.where(odd == 1, high, jnp.minimum((s + 1) * PIECES, pieces)))

        @pl.when((j >= 2) & (j < nz - 3))
        def _():
            pass_on(chip_of(j - 2))

        @pl.when(j == nz - 4)
        def _():
            pass_on(chip_of(j - 1))
            lax.fori_loop(nz - 5, nz - 3, settle, 0)
            for i in range(ny):
                H[i] = R[:, i * slab : (i + 1) * slab]
            R[...] = jnp.zeros_like(R)
            RY[y] = H[y]
            for d in far_first(ny):
                dst = lax.rem(y + d, ny)
                to_y("ry", H.at[dst], RY.at[y], d).start()

        return 0

    lax.fori_loop(1, nz - 1, turn, 0)
    for j in (nz - 3, nz - 2):
        need_ct(chip_of(j))
        scale_sum(chip_of(j))
    need_tokens(nz - 1)
    project(chip_of(nz - 1))

    need_ct(chip_of(nz - 1))
    scale_sum(chip_of(nz - 1))
    me = y * nx + x
    SS[me] = jnp.sum(SACC[...], axis=0, keepdims=True)
    away = [(dy, dx) for dy in range(ny) for dx in range(nx) if dy or dx]
    for dy, dx in sorted(away, key=lambda o: -min(o[0], ny - o[0]) - min(o[1], nx - o[1])):
        dev = (lax.rem(y + dy, ny), lax.rem(x + dx, nx), z, k)
        copy(SS.at[me], SS.at[me], leave("s"), enter("s"), dev).start()

    def finish_b(j, _):
        backward(chip_of(j))
        return 0

    lax.fori_loop(nz - 3, nz, finish_b, 0)
    for i in range(ny):
        HL[i] = R[:, i * slab : (i + 1) * slab].astype(BF16)
    RL[y] = HL[y]
    for d in far_first(ny):
        dst = lax.rem(y + d, ny)
        to_y("rl", HL.at[dst], RL.at[y], d).start()
    for i in range(nx):
        BGS[i] = BG[:, i * part : (i + 1) * part]
    BX[x] = BGS[x]

    for d in range(1, nx):
        dst = lax.rem(x + d, nx)
        to_x("bx", BGS.at[dst], BX.at[x], d).start()

    def send_held(j, _):
        send_p(chip_of(j))
        return 0

    lax.fori_loop(held, nz, send_held, 0)
    pass_on(chip_of(held - 1))

    arrived(enter("ry"), RY.at[pl.ds(0, ny - 1)])
    row_part = RY[0]
    for i in range(1, ny):
        row_part = row_part + RY[i]
    norm = NORM[...]
    inverse = 1.0 / norm
    slope = -MAG[...] * (inverse * inverse * inverse)

    arrived(enter("s"), SS.at[pl.ds(0, nx * ny - 1)])
    s_all = SS[0]
    for i in range(1, nx * ny):
        s_all = s_all + SS[i]
    coef = s_all * slope
    scaled = (B[...].astype(F32) * coef).astype(BF16)
    part_y = nn(jnp.concatenate([scaled] * 3, axis=1), WX[...])
    arrived(enter("rl"), RL.at[pl.ds(0, ny - 1)])
    for i in range(ny):
        row_part = row_part + RL[i].astype(F32)
    part_y = part_y + row_part

    for i in range(2):
        CX[i] = part_y[:, i * lane : (i + 1) * lane].astype(BF16)
    here = 2 * z + k
    ZX[here] = CX[k]
    for d in far_first(nz) + [0]:
        for other in (0, 1):
            if d or other:
                core = k if other == 0 else 1 - k
                dev = (y, x, lax.rem(z + d, nz), core)
                copy(CX.at[core], ZX.at[here], leave("zx"), enter("zx"), dev).start()
    gmag_ref[...] = s_all * inverse

    def pass_held(j, _):
        pass_on(chip_of(j))
        return 0


    arrived(enter("bx"), BX.at[pl.ds(0, nx - 1)])
    bx = BX[0]
    for i in range(1, nx):
        bx = bx + BX[i]
    BY[y] = bx
    for d in far_first(ny):
        to_y("by", BY.at[y], BY.at[y], d).start()
    lax.fori_loop(held, nz, pass_held, 0)
    arrived(enter("ax"), AX.at[pl.ds(0, nx - 1)])
    a_all = AX[0]
    for i in range(1, nx):
        a_all = a_all + AX[i]

    arrived(enter("zx"), ZX.at[pl.ds(0, 2 * nz - 1)])
    whole = ZX[0].astype(F32)
    for i in range(1, 2 * nz):
        whole = whole + ZX[i].astype(F32)
    spot = 2 * y + k
    IF[spot] = whole.astype(BF16)
    for d in far_first(ny) + [0]:
        for other in (0, 1):
            if d or other:
                dev = (lax.rem(y + d, ny), x, z, k if other == 0 else 1 - k)
                copy(IF.at[spot], IF.at[spot], leave("if"), enter("if"), dev).start()

    arrived(enter("p"), PR)
    rest = pl.ds(pl.multiple_of(x * own, own), own)
    total = PF[rest, :]
    for side in range(2):
        total = total + PR[side].astype(F32)
    proj_ref[...] = (total * SCALE[...]).astype(BF16)

    arrived(enter("by"), BY.at[pl.ds(0, ny - 1)])
    b_all = BY[0]
    for i in range(1, ny):
        b_all = b_all + BY[i]

    for i in range(nx):

        @pl.when(x == i)
        def _():
            c = slice(i * part, (i + 1) * part)
            gb_ref[:, c] = b_all + a_all * coef[:, c]

    def gb_part(i):
        return gb_ref.at[:, pl.ds(pl.multiple_of(i * part, part), part)]

    for d in range(1, nx):
        to_x("bo", gb_part(x), gb_part(x), d).start()

    arrived(enter("bo"), gb_ref.at[:, pl.ds(0, (nx - 1) * part)])
    arrived(enter("if"), IF.at[pl.ds(0, 2 * ny - 1)])
    for i in range(2 * ny):
        ifg_ref[:, i * lane : (i + 1) * lane] = IF[i].astype(F32)

    def sent(name, ref):
        copy(ref, ref, leave(name), leave(name), partner).wait_send()

    sent("zr", T.at[pl.ds(0, pieces * piece)])
    sent("zl", T.at[pl.ds(0, pieces * piece)])
    sent("d", T.at[pl.ds(0, 2 * pieces * piece)])
    sent("own", T.at[pl.ds(0, rows)])
    sent("ct", CT.at[pl.ds(0, (nx - 1) * own)])
    sent("p", PS.at[pl.ds(0, (nx - 1) * own)])
    sent("nx", NX.at[pl.ds(0, nx - 1)])
    sent("ax", AX.at[pl.ds(0, nx - 1)])
    sent("s", SS.at[pl.ds(0, nx * ny - 1)])
    sent("bx", BX.at[pl.ds(0, nx - 1)])
    sent("by", BY.at[pl.ds(0, ny - 1)])
    sent("bo", gb_ref.at[:, pl.ds(0, (nx - 1) * part)])
    sent("ry", RY.at[pl.ds(0, ny - 1)])
    sent("rl", RL.at[pl.ds(0, ny - 1)])
    sent("zx", ZX.at[pl.ds(0, 2 * nz - 1)])
    sent("if", IF.at[pl.ds(0, 2 * ny - 1)])


def put_out(*refs):
    *pairs, sem = refs
    copies = [pltpu.make_async_copy(pairs[i], pairs[i + 4], sem.at[i]) for i in range(4)]
    for c in copies:
        c.start()
    for c in copies:
        c.wait()


def per_device(sizes, tokens, weight, a, b, magnitude, cotangent, lengths):
    ny, nx, nz = sizes
    rows, feats = tokens.shape
    rank, cols = b.shape
    group = rows * 2 * nz
    own = group // nx
    slab = feats // ny
    part = cols // nx
    per = nz // nx
    ring = (nz // 2 - 1) * PIECES + PIECES // 2
    words = ny // 2 + nx // 2 + nz // 2 - 2
    V = pltpu.VMEM
    S = lambda n: pltpu.SemaphoreType.DMA((n,))
    outs = pl.pallas_call(
        functools.partial(kernel, sizes),
        out_shape=(
            V((own, cols), BF16),
            V((1, cols), F32),
            V((rank, feats), F32),
            V((rank, cols), F32),
        ),
        in_specs=[pl.BlockSpec(memory_space=pl.ANY)] * 7,
        out_specs=[pl.BlockSpec(memory_space=pltpu.VMEM)] * 4,
        scratch_shapes=[
            V((group, feats), BF16),
            V((feats, cols), BF16),
            V((rank, feats), BF16),
            V((rank, cols), BF16),
            V((group, cols), BF16),
            V((group, 128), F32),
            V((group, cols), F32),
            V((group, cols), BF16),
            V((2, own, cols), BF16),
            V((own, cols), BF16),
            V((group, rank), BF16),
            V((nx, 1, cols), F32),
            V((nx, rank, part), F32),
            V((8, cols), F32),
            V((nx * ny, 1, cols), F32),
            V((1, cols), F32),
            V((1, cols), F32),
            V((rank, cols), F32),
            V((nx, rank, part), F32),
            V((nx, rank, part), F32),
            V((ny, rank, part), F32),
            V((rank, feats), F32),
            V((ny, rank, slab), F32),
            V((ny, rank, slab), F32),
            V((ny, rank, slab), BF16),
            V((ny, rank, slab), BF16),
            V((2, rank, slab // 2), BF16),
            V((2 * nz, rank, slab // 2), BF16),
            V((2 * ny, rank, slab // 2), BF16),
            V((nx, rank, part), F32),
            V((3 * cols, slab), BF16),
            V((1, cols), F32),
            pltpu.SMEM(lengths.shape, jnp.int32),
            S(7),
            S(ring), S(ring),
            S(nz), S(nz), S(per),
            S(len(LEAVE)), S(len(ENTER)),
            pltpu.SemaphoreType.REGULAR((words,)),
        ],
        compiler_params=pltpu.CompilerParams(
            collective_id=0, has_side_effects=True, vmem_limit_bytes=56 * 1024 * 1024
        ),
        name="lora_step",
    )(tokens, weight, a, b, magnitude.reshape(1, cols), cotangent, lengths)
    whole = [jax.ShapeDtypeStruct(o.shape, o.dtype) for o in outs]
    proj, gmag, ifg, gb = pl.pallas_call(
        put_out,
        out_shape=whole,
        in_specs=[pl.BlockSpec(memory_space=pltpu.VMEM)] * 4,
        out_specs=[pl.BlockSpec(memory_space=pl.ANY)] * 4,
        scratch_shapes=[S(4)],
        compiler_params=pltpu.CompilerParams(vmem_limit_bytes=1024 * 1024),
        name="put_out",
    )(*outs)
    return proj, gmag.reshape(cols), ifg, gb


def solution(mesh):
    ny, nx = mesh.shape["dp"], mesh.shape["row"]
    nz = mesh.shape["col"] // 2
    split = Mesh(mesh.devices.reshape(ny, nx, nz, 2), AXES)
    return jax.shard_map(
        functools.partial(per_device, (ny, nx, nz)),
        mesh=split,
        in_specs=(
            P(("dp", "z", "core"), "row"),
            P("row", COL),
            P(None, "row"),
            P(None, COL),
            P(COL),
            P(("dp", "row"), COL),
            P("dp", None),
        ),
        out_specs=(P(("dp", "row"), COL), P(COL), P(None, "row"), P(None, COL)),
        check_vma=False,
    )
```

time: 65.4 us -> 57.7 us (0.88)
  the two profiles are of different devices: /device:TPU:5 before, /device:TPU:1 now
where the time goes in v3:
time: 57.7 us; the launch traced here: 57.5 us
  Pallas kernels  56.9 us (99%)
  between operations  0.64 us (1%)
    pallas_call x1, Pallas kernels, per_device(): pl.pallas_call(functools.partial(kernel, sizes), out_shape=(V((own, cols)...  56.1 us

profile of v3, /device:TPU:1, one launch (start us, length us, event | category | flops | bytes accessed | tf_op | source)
XLA Modules:
  0.0 57.5 jit_solution(16430830747241833243)
XLA Ops:
  0.6 56.1 %lora_step.1 = (bf16[256,512]{1,0:T(8,128)(2,1)S(1)}, f32[1,512]{1,0:T(1,128)S(1)}, f32[16,2048]{1,0:T(8,128)S(1)}, f32[16,512]{1,0:T(8,128)S(1)}) custom-call(bf16[64,2048]{1,0:T(8,128)(2,1)} %tok_hbm.1, bf16[2048,512]{1,0:T(8,128)(2,1)} %w_hbm.1, bf16[16,2048]{1,0:T(8,128)(2,1)} %a_hbm.1, bf16[16,512]{1,0:T(8,128)(2,1)} %b_hbm.1, f32[1,512]{1,0:T(1,128)} %bitcast.2, ...), custom_call_target="tpu_custom_call" | custom-call | tf_op jit(solution)/shard_map/lora_step/pallas_call | solution.py:613
  56.7 0.8 %put_out.1 = (bf16[256,512]{1,0:T(8,128)(2,1)}, f32[1,512]{1,0:T(1,128)}, f32[16,2048]{1,0:T(8,128)}, f32[16,512]{1,0:T(8,128)}) custom-call(bf16[256,512]{1,0:T(8,128)(2,1)S(1)} %get-tuple-element.12.refs_0_, f32[1,512]{1,0:T(1,128)S(1)} %get-tuple-element.13.refs_1_, f32[16,2048]{1,0:T(8,128)S(1)} %get-tuple-element.14.refs_2_, ...), custom_call_target="tpu_custom_call" | custom-call | tf_op jit(solution)/shard_map/put_out/pallas_call | solution.py:669

commit v4 on v3

--- a/solution.py
+++ b/solution.py
@@ -19,7 +19,9 @@
 EARLY = 6
 
 
-LEAVE = ("zr", "zl", "d", "own", "ct", "p", "nx", "ax", "s", "bx", "by", "bo", "ry", "rl", "zx", "if")
+TOKEN = "own"
+SAME = ("zr", "zl", "d", "own")
+LEAVE = ("own", "ct", "p", "nx", "ax", "s", "bx", "by", "bo", "ry", "rl", "zx", "if")
 ENTER = ("p", "nx", "ax", "s", "bx", "by", "bo", "ry", "rl", "zx", "if")
 
 
@@ -75,7 +77,7 @@
         return at(axis, lax.rem((y, x, z)[axis] + by + n, n))
 
     def leave(name):
-        return out_sem.at[LEAVE.index(name)]
+        return out_sem.at[LEAVE.index(TOKEN if name in SAME else name)]
 
     def enter(name):
         return in_sem.at[ENTER.index(name)]
@@ -93,31 +95,36 @@
     def arrived(sem, ref):
         copy(ref, ref, sem, sem, partner).wait_recv()
 
-    barrier = pltpu.get_barrier_semaphore()
-    near = [partner] + [step(axis, d, n) for axis, n in ((2, nz), (1, nx), (0, ny)) for d in (1, -1)]
-
-    def signal(sem, dev):
-        pl.semaphore_signal(sem, inc=1, device_id=dev, device_id_type=pl.DeviceIdType.MESH)
-
-    for dev in near:
-        signal(barrier, dev)
-
     def token_rows(chip, core, h, n):
         return pl.ds(pl.multiple_of(chip * unit + core * rows + h * piece, piece), n)
 
     mine = token_rows(z, k, 0, rows)
     owned = pl.ds(pl.multiple_of(x * own, own), own)
     loads = [
-        pltpu.make_async_copy(tok_hbm, T.at[mine], load_sem.at[0]),
-        pltpu.make_async_copy(ct_hbm, CT.at[owned], load_sem.at[1]),
-        pltpu.make_async_copy(a_hbm, A, load_sem.at[2]),
-        pltpu.make_async_copy(b_hbm, B, load_sem.at[3]),
-        pltpu.make_async_copy(w_hbm, W, load_sem.at[4]),
-        pltpu.make_async_copy(mag_hbm, MAG, load_sem.at[5]),
-        pltpu.make_async_copy(lens_hbm, LENS, load_sem.at[6]),
+        pltpu.make_async_copy(ct_hbm, CT.at[owned], load_sem.at[0]),
+        pltpu.make_async_copy(a_hbm, A, load_sem.at[1]),
+        pltpu.make_async_copy(b_hbm, B, load_sem.at[2]),
+        pltpu.make_async_copy(w_hbm, W, load_sem.at[3]),
+        pltpu.make_async_copy(mag_hbm, MAG, load_sem.at[4]),
+        pltpu.make_async_copy(lens_hbm, LENS, load_sem.at[5]),
     ]
-    for c in loads:
+    first = [
+        pltpu.make_async_copy(
+            tok_hbm.at[pl.ds(h * piece, piece)], T.at[token_rows(z, k, h, piece)], load_sem.at[6 + h]
+        )
+        for h in range(PIECES)
+    ]
+    for c in first + loads:
         c.start()
+
+    barrier = pltpu.get_barrier_semaphore()
+    near = [partner] + [step(axis, d, n) for axis, n in ((2, nz), (1, nx), (0, ny)) for d in (1, -1)]
+
+    def signal(sem, dev):
+        pl.semaphore_signal(sem, inc=1, device_id=dev, device_id_type=pl.DeviceIdType.MESH)
+
+    for dev in near:
+        signal(barrier, dev)
 
     seqs = LENS.shape[1]
 
@@ -134,7 +141,6 @@
         WT[pl.ds(pl.multiple_of(i * unit, unit), unit), :] = total
         return 0
 
-    loads[0].wait()
     pl.semaphore_wait(barrier, len(near))
 
     def ring(right_way, src_chip, h, idx):
@@ -150,6 +156,7 @@
     full = (nz // 2 - 1) * PIECES
     pieces = full + PIECES // 2
     for h in range(PIECES):
+        first[h].wait()
         ring(True, z, h, h).start()
         ring(False, z, h, h).start()
     copy(T.at[mine], T.at[mine], leave("own"), d_r.at[0], partner).start()
@@ -166,7 +173,7 @@
 
     tell(1, 0)
     tell(2, 0)
-    loads[6].wait()
+    loads[5].wait()
     lax.fori_loop(0, nz, weigh, 0)
     def spread_word(level):
         for axis in (0, 2):
@@ -202,7 +209,7 @@
         ct_copy(loc, m // (nx - 1), lax.rem(x + 1 + lax.rem(m, nx - 1), nx), x).start()
         return 0
 
-    for c in loads[2:6]:
+    for c in loads[1:5]:
         c.wait()
     chunk = slab
 
@@ -218,7 +225,7 @@
         if level + 1 < levels[1]:
             tell(1, level + 1)
     tell(0, 0)
-    loads[1].wait()
+    loads[0].wait()
 
     def to_x(name, src, slot, d):
         return copy(src, slot, leave(name), enter(name), step(1, d, nx))
@@ -377,7 +384,7 @@
         odd = lax.rem(j, 2)
         chip = chip_of(j)
 
-        @pl.when(odd == 1)
+        @pl.when((odd == 1) & (j < nz - 3))
         def _():
             handle(s * PIECES)
 
@@ -395,8 +402,10 @@
             SCALE[...] = MAG[...] / norm
 
         mid = s * PIECES + PIECES // 2
-        low = jnp.minimum(jnp.where(odd == 1, s * PIECES + 1, mid), pieces)
-        high = jnp.minimum(jnp.where(odd == 1, mid, mid + 1), pieces)
+        low = jnp.minimum(jnp.where(odd == 1, s * PIECES + 1, mid), full)
+        high = jnp.minimum(jnp.where(odd == 1, mid, mid + 1), full)
+        low = jnp.where(j == nz - 3, full, low)
+        high = jnp.where(j == nz - 3, pieces, high)
         handle_range(low, high)
 
         for level in range(max(levels.values())):
@@ -413,7 +422,7 @@
         def _():
             settle(j - 2, 0)
 
-        handle_range(high, jnp.where(odd == 1, high, jnp.minimum((s + 1) * PIECES, pieces)))
+        handle_range(high, jnp.where(odd == 1, high, jnp.minimum((s + 1) * PIECES, full)))
 
         @pl.when((j >= 2) & (j < nz - 3))
         def _():
@@ -421,7 +430,6 @@
 
         @pl.when(j == nz - 4)
         def _():
-            pass_on(chip_of(j - 1))
             lax.fori_loop(nz - 5, nz - 3, settle, 0)
             for i in range(ny):
                 H[i] = R[:, i * slab : (i + 1) * slab]
@@ -473,7 +481,8 @@
         return 0
 
     lax.fori_loop(held, nz, send_held, 0)
-    pass_on(chip_of(held - 1))
+    for j in (held - 2, held - 1):
+        pass_on(chip_of(j))
 
     arrived(enter("ry"), RY.at[pl.ds(0, ny - 1)])
     row_part = RY[0]
@@ -570,10 +579,7 @@
     def sent(name, ref):
         copy(ref, ref, leave(name), leave(name), partner).wait_send()
 
-    sent("zr", T.at[pl.ds(0, pieces * piece)])
-    sent("zl", T.at[pl.ds(0, pieces * piece)])
-    sent("d", T.at[pl.ds(0, 2 * pieces * piece)])
-    sent("own", T.at[pl.ds(0, rows)])
+    sent("own", T.at[pl.ds(0, 4 * pieces * piece + rows)])
     sent("ct", CT.at[pl.ds(0, (nx - 1) * own)])
     sent("p", PS.at[pl.ds(0, (nx - 1) * own)])
     sent("nx", NX.at[pl.ds(0, nx - 1)])
@@ -654,7 +660,7 @@
             V((3 * cols, slab), BF16),
             V((1, cols), F32),
             pltpu.SMEM(lengths.shape, jnp.int32),
-            S(7),
+            S(6 + PIECES),
             S(ring), S(ring),
             S(nz), S(nz), S(per),
             S(len(LEAVE)), S(len(ENTER)),

time: 57.7 us -> 57.3 us (level)
  no operation moved by 1% of the time
where the time goes in v4:
time: 57.3 us; the launch traced here: 57.1 us
  Pallas kernels  56.5 us (99%)
  between operations  0.64 us (1%)
    pallas_call x1, Pallas kernels, per_device(): pl.pallas_call(functools.partial(kernel, sizes), out_shape=(V((own, cols)...  55.7 us

profile of v4, /device:TPU:1, one launch (start us, length us, event | category | flops | bytes accessed | tf_op | source)
XLA Modules:
  0.0 57.1 jit_solution(2342470767566125024)
XLA Ops:
  0.6 55.7 %lora_step.1 = (bf16[256,512]{1,0:T(8,128)(2,1)S(1)}, f32[1,512]{1,0:T(1,128)S(1)}, f32[16,2048]{1,0:T(8,128)S(1)}, f32[16,512]{1,0:T(8,128)S(1)}) custom-call(bf16[64,2048]{1,0:T(8,128)(2,1)} %tok_hbm.1, bf16[2048,512]{1,0:T(8,128)(2,1)} %w_hbm.1, bf16[16,2048]{1,0:T(8,128)(2,1)} %a_hbm.1, bf16[16,512]{1,0:T(8,128)(2,1)} %b_hbm.1, f32[1,512]{1,0:T(1,128)} %bitcast.2, ...), custom_call_target="tpu_custom_call" | custom-call | tf_op jit(solution)/shard_map/lora_step/pallas_call | solution.py:619
  56.4 0.8 %put_out.1 = (bf16[256,512]{1,0:T(8,128)(2,1)}, f32[1,512]{1,0:T(1,128)}, f32[16,2048]{1,0:T(8,128)}, f32[16,512]{1,0:T(8,128)}) custom-call(bf16[256,512]{1,0:T(8,128)(2,1)S(1)} %get-tuple-element.12.refs_0_, f32[1,512]{1,0:T(1,128)S(1)} %get-tuple-element.13.refs_1_, f32[16,2048]{1,0:T(8,128)S(1)} %get-tuple-element.14.refs_2_, ...), custom_call_target="tpu_custom_call" | custom-call | tf_op jit(solution)/shard_map/put_out/pallas_call | solution.py:675

commit v5 on v4

--- a/solution.py
+++ b/solution.py
@@ -56,7 +56,7 @@
     tok_hbm, w_hbm, a_hbm, b_hbm, mag_hbm, ct_hbm, lens_hbm,
     proj_ref, gmag_ref, ifg_ref, gb_ref,
     T, W, A, B, CT, WT, PF, PS, PR, PV, DB,
-    NX, AX, SACC, SS, SCALE, NORM, BG, BGS, BX, BY, R, RY, H, RL, HL, CX, ZX, IF, AM, WX, MAG, LENS,
+    NX, AX, SACC, SS, SCALE, NORM, BG, BGS, BX, BY, R, RY, H, RL, HL, CX, ZX, IF, AM, WX, AT, MAG, LENS,
     load_sem, zr_r, zl_r, d_r, ct_r, pv_r, out_sem, in_sem, wave,
 ):
     ny, nx, nz = sizes
@@ -157,8 +157,19 @@
     pieces = full + PIECES // 2
     for h in range(PIECES):
         first[h].wait()
-        ring(True, z, h, h).start()
-        ring(False, z, h, h).start()
+        if h < PIECES // 2:
+            ring(True, z, h, h).start()
+            ring(False, z, h, h).start()
+
+    def rest_of_own():
+        for h in range(PIECES // 2, PIECES):
+            ring(True, z, h, h).start()
+            ring(False, z, h, h).start()
+
+    @pl.when(k == 0)
+    def _():
+        rest_of_own()
+
     copy(T.at[mine], T.at[mine], leave("own"), d_r.at[0], partner).start()
 
     levels = {0: ny // 2, 1: nx // 2 - 1, 2: nz // 2 - 1}
@@ -175,6 +186,11 @@
     tell(2, 0)
     loads[5].wait()
     lax.fori_loop(0, nz, weigh, 0)
+
+    @pl.when(k == 1)
+    def _():
+        rest_of_own()
+
     def spread_word(level):
         for axis in (0, 2):
             if level < levels[axis]:
@@ -237,6 +253,8 @@
         to_x("nx", NX.at[x], NX.at[x], d).start()
     lax.fori_loop(0, EARLY, send_ct, 0)
 
+    wide_a = jnp.concatenate([A[...].astype(F32), jnp.zeros((128 - A.shape[0], A.shape[1]), F32)], axis=0)
+    AT[...] = wide_a.T.astype(BF16)
     SACC[...] = jnp.zeros_like(SACC)
     BG[...] = jnp.zeros_like(BG)
     R[...] = jnp.zeros_like(R)
@@ -253,7 +271,7 @@
     def project(chip):
         r = unit_rows(chip)
         t = T[r, :]
-        down = nt(t, A[...]).astype(BF16)
+        down = nn(t, AT[...])[:, : A.shape[0]].astype(BF16)
         p = nn(t, W[...]) + nn(down, B[...])
         DB[r, :] = down
         PF[r, :] = p
@@ -658,6 +676,7 @@
             V((2 * ny, rank, slab // 2), BF16),
             V((nx, rank, part), F32),
             V((3 * cols, slab), BF16),
+            V((feats, 128), BF16),
             V((1, cols), F32),
             pltpu.SMEM(lengths.shape, jnp.int32),
             S(6 + PIECES),

time: 57.3 us -> 56.7 us (0.990)
  Pallas kernels: 56.5 us -> 55.9 us
    pallas_call x1, Pallas kernels: 55.7 us -> 55.1 us  [per_device(): pl.pallas_call(functools.partial(kernel, sizes), out_shape=(V((own, cols)...]
where the time goes in v5:
time: 56.7 us; the launch traced here: 56.6 us
  Pallas kernels  55.9 us (99%)
  between operations  0.64 us (1%)
    pallas_call x1, Pallas kernels, per_device(): pl.pallas_call(functools.partial(kernel, sizes), out_shape=(V((own, cols)...  55.1 us

profile of v5, /device:TPU:1, one launch (start us, length us, event | category | flops | bytes accessed | tf_op | source)
XLA Modules:
  0.0 56.6 jit_solution(5666751072225779745)
XLA Ops:
  0.6 55.1 %lora_step.1 = (bf16[256,512]{1,0:T(8,128)(2,1)S(1)}, f32[1,512]{1,0:T(1,128)S(1)}, f32[16,2048]{1,0:T(8,128)S(1)}, f32[16,512]{1,0:T(8,128)S(1)}) custom-call(bf16[64,2048]{1,0:T(8,128)(2,1)} %tok_hbm.1, bf16[2048,512]{1,0:T(8,128)(2,1)} %w_hbm.1, bf16[16,2048]{1,0:T(8,128)(2,1)} %a_hbm.1, bf16[16,512]{1,0:T(8,128)(2,1)} %b_hbm.1, f32[1,512]{1,0:T(1,128)} %bitcast.2, ...), custom_call_target="tpu_custom_call" | custom-call | tf_op jit(solution)/shard_map/lora_step/pallas_call | solution.py:637
  55.8 0.8 %put_out.1 = (bf16[256,512]{1,0:T(8,128)(2,1)}, f32[1,512]{1,0:T(1,128)}, f32[16,2048]{1,0:T(8,128)}, f32[16,512]{1,0:T(8,128)}) custom-call(bf16[256,512]{1,0:T(8,128)(2,1)S(1)} %get-tuple-element.12.refs_0_, f32[1,512]{1,0:T(1,128)S(1)} %get-tuple-element.13.refs_1_, f32[16,2048]{1,0:T(8,128)S(1)} %get-tuple-element.14.refs_2_, ...), custom_call_target="tpu_custom_call" | custom-call | tf_op jit(solution)/shard_map/put_out/pallas_call | solution.py:694

commit v6 on v5

--- a/solution.py
+++ b/solution.py
@@ -16,7 +16,7 @@
 HIGHEST = lax.Precision.HIGHEST
 HELD = 5
 PIECES = 4
-EARLY = 6
+EARLY = 4
 
 
 TOKEN = "own"

time: 56.7 us -> 56.3 us (level)
  no operation moved by 1% of the time
where the time goes in v6:
time: 56.3 us; the launch traced here: 56.2 us
  Pallas kernels  55.5 us (99%)
  between operations  0.64 us (1%)
    pallas_call x1, Pallas kernels, per_device(): pl.pallas_call(functools.partial(kernel, sizes), out_shape=(V((own, cols)...  54.7 us

profile of v6, /device:TPU:1, one launch (start us, length us, event | category | flops | bytes accessed | tf_op | source)
XLA Modules:
  0.0 56.2 jit_solution(18221417127310890210)
XLA Ops:
  0.6 54.7 %lora_step.1 = (bf16[256,512]{1,0:T(8,128)(2,1)S(1)}, f32[1,512]{1,0:T(1,128)S(1)}, f32[16,2048]{1,0:T(8,128)S(1)}, f32[16,512]{1,0:T(8,128)S(1)}) custom-call(bf16[64,2048]{1,0:T(8,128)(2,1)} %tok_hbm.1, bf16[2048,512]{1,0:T(8,128)(2,1)} %w_hbm.1, bf16[16,2048]{1,0:T(8,128)(2,1)} %a_hbm.1, bf16[16,512]{1,0:T(8,128)(2,1)} %b_hbm.1, f32[1,512]{1,0:T(1,128)} %bitcast.2, ...), custom_call_target="tpu_custom_call" | custom-call | tf_op jit(solution)/shard_map/lora_step/pallas_call | solution.py:637
  55.4 0.8 %put_out.1 = (bf16[256,512]{1,0:T(8,128)(2,1)}, f32[1,512]{1,0:T(1,128)}, f32[16,2048]{1,0:T(8,128)}, f32[16,512]{1,0:T(8,128)}) custom-call(bf16[256,512]{1,0:T(8,128)(2,1)S(1)} %get-tuple-element.12.refs_0_, f32[1,512]{1,0:T(1,128)S(1)} %get-tuple-element.13.refs_1_, f32[16,2048]{1,0:T(8,128)S(1)} %get-tuple-element.14.refs_2_, ...), custom_call_target="tpu_custom_call" | custom-call | tf_op jit(solution)/shard_map/put_out/pallas_call | solution.py:694
